TPU v7x, 32 devices: a whole 2x2x4 slice. The times are simulated.
32 devices in a mesh: gx: 8 (over z, y), gy: 4 (over x, core).
Axes of the slice: x: 2, y: 2, z: 4, core: 2. Of those that a mesh axis runs over, the one named last changes fastest.
Arguments:
- liquid_starting_warmth: float32 [32, 64, 1024], P('gx', 'gy'), may hold values from -6 to 6
- liquid_spreading_ratios: float32 [32, 64, 1024], P('gx', 'gy'), may hold values from 0.02 to 0.12
- liquid_advective_ratios: float32 [3, 32, 64, 1024], P(None, 'gx', 'gy'), may hold values from -0.08 to 0.08
- liquid_refresh_flags: int32 [32, 64, 8], P('gx', 'gy'), may hold values 0 or 1
- wall_starting_warmth: float32 [32, 64, 1024], P('gx', 'gy'), may hold values from -6 to 6
- wall_thermal_capacity: float32 [32, 64, 1024], P('gx', 'gy'), may hold values from 0.5 to 2
- thermal_conductance: float32 [32, 64, 1024], P('gx', 'gy'), may hold values from 0.5 to 15
- wall_energy_output: float32 [32, 64, 1024], P('gx', 'gy'), may hold values from -36 to 36
- coupling_partner_lookup: int32 [32, 64], P('gx', 'gy'), may hold values from 0 to 63, each once within a row
Outputs:
- fluid_after: float32 [32, 64, 1024], P('gx', 'gy')
- solid_after: float32 [32, 64, 1024], P('gx', 'gy')
Inputs may be any that keep to these rules, and one draw needn't show every extreme that they name: For each first index, the row of coupling_partner_lookup holds every number of 0 to 63 once.
All inputs are finite; a program needn't handle non-finite values. No bound on the sum of `liquid_refresh_flags` on one device may be relied on, other than what follows from the above.
Results may differ from a plain program's by a relative error of at most 0.00023.
Values sent between devices are 32-bit elements; how exact they have to be, the bound alone decides.
A program may use at most 64 MiB of HBM per device.

v0:
```python
import jax
import jax.numpy as jnp
from jax import lax
from jax.sharding import PartitionSpec as P

SUBSTEPS = 4
ITERS = 4
ZB = 128


def padded_2(cells, sides, width):
    for axis, dim in sides:
        count = lax.axis_size(axis)
        ends = count - 1
        head = lax.slice_in_dim(cells, 0, width, axis=dim)
        tail = lax.slice_in_dim(cells, cells.shape[dim] - width, cells.shape[dim], axis=dim)
        cells = jnp.concatenate(
            [
                lax.ppermute(tail, axis, [(i, (i + 1) % count) for i in range(ends)]),
                cells,
                lax.ppermute(head, axis, [((i + 1) % count, i) for i in range(ends)]),
            ],
            axis=dim,
        )
    return cells


def advance(current_estimate, padded, ghost_row, diffusion, velocity, active_cells):
    below = jnp.concatenate([ghost_row[:, :, None], current_estimate[:, :, :-1]], axis=2)
    above = jnp.concatenate(
        [current_estimate[:, :, 1:], jnp.zeros_like(current_estimate[:, :, :1])], axis=2
    )
    couples = (
        (padded[:-2, 1:-1], padded[2:, 1:-1]),
        (padded[1:-1, :-2], padded[1:-1, 2:]),
        (below, above),
    )
    spread = -6.0 * current_estimate
    carried = jnp.zeros_like(current_estimate)
    for component in range(3):
        behind, ahead = couples[component]
        spread = spread + behind + ahead
        flow_speed = velocity[component]
        carried = (
            carried
            + jnp.maximum(flow_speed, 0.0) * (current_estimate - behind)
            + jnp.minimum(flow_speed, 0.0) * (ahead - current_estimate)
        )
    return current_estimate + active_cells * (diffusion * spread - carried)


def neighbours(field, padded):
    below = jnp.concatenate([jnp.zeros_like(field[:, :, :1]), field[:, :, :-1]], axis=2)
    above = jnp.concatenate([field[:, :, 1:], jnp.zeros_like(field[:, :, :1])], axis=2)
    return (padded[:-2, 1:-1], padded[2:, 1:-1], padded[1:-1, :-2], padded[1:-1, 2:], below, above)


def thermal_flow_operator(field, padded_field, thermal_conductance, bordered_conductance, capacity):
    accumulated = capacity * field
    for near_value, near_cond in zip(
        neighbours(field, padded_field), neighbours(thermal_conductance, bordered_conductance)
    ):
        accumulated = accumulated + 0.5 * (thermal_conductance + near_cond) * (field - near_value)
    return accumulated


def diagonal_of(thermal_conductance, bordered_conductance, capacity):
    accumulated = capacity
    for near_cond in neighbours(thermal_conductance, bordered_conductance):
        accumulated = accumulated + 0.5 * (thermal_conductance + near_cond)
    return accumulated


def local(
    liquid_starting_warmth,
    liquid_spreading_ratios,
    liquid_advective_ratios,
    liquid_refresh_flags,
    wall_starting_warmth,
    wall_thermal_capacity,
    thermal_conductance,
    wall_energy_output,
    coupling_partner_lookup,
):
    local_cols = coupling_partner_lookup.shape[1]
    topmost_layers = lax.all_gather(wall_starting_warmth[:, :, -1], "gy", axis=1, tiled=True)
    positions = jnp.arange(topmost_layers.shape[1], dtype=jnp.int32)
    picks = coupling_partner_lookup[:, :, None] == positions[None, None, :]
    ghost_row = jnp.sum(jnp.where(picks, topmost_layers[:, None, :], 0.0), axis=2)
    active_cells = jnp.repeat(liquid_refresh_flags.astype(jnp.float32), ZB, axis=2)
    padded_fluid, bordered_wall_warmth, bordered_conductance = (
        padded_2(liquid_starting_warmth, (("gx", 0), ("gy", 1)), 1),
        padded_2(wall_starting_warmth, (("gx", 0), ("gy", 1)), 1),
        padded_2(thermal_conductance, (("gx", 0), ("gy", 1)), 1),
    )
    current_estimate = liquid_starting_warmth
    padded = padded_fluid
    flux_sum = jnp.zeros_like(ghost_row)
    for substep in range(SUBSTEPS):
        flux_sum = flux_sum + (current_estimate[:, :, 0] - ghost_row)
        if substep > 0:
            padded = padded_2(current_estimate, (("gx", 0), ("gy", 1)), 1)
        current_estimate = advance(
            current_estimate,
            padded,
            ghost_row,
            liquid_spreading_ratios,
            liquid_advective_ratios,
            active_cells,
        )
    flux_mean = flux_sum / SUBSTEPS
    map_wide = lax.all_gather(coupling_partner_lookup, "gy", axis=1, tiled=True)
    flux_wide = lax.all_gather(flux_mean, "gy", axis=1, tiled=True)
    own_cols = lax.axis_index("gy") * local_cols + jnp.arange(local_cols, dtype=jnp.int32)
    owners = map_wide[:, None, :] == own_cols[None, :, None]
    arrived = jnp.sum(jnp.where(owners, flux_wide[:, None, :], 0.0), axis=2)
    equation_source_term = wall_thermal_capacity * wall_starting_warmth + wall_energy_output
    equation_source_term = equation_source_term.at[:, :, -1].add(arrived)
    diagonal = diagonal_of(thermal_conductance, bordered_conductance, wall_thermal_capacity)

    def apply_stiffness_matrix(field, padded_field):
        return thermal_flow_operator(
            field, padded_field, thermal_conductance, bordered_conductance, wall_thermal_capacity
        )

    def rimmed(field):
        return padded_2(field, (("gx", 0), ("gy", 1)), 1)

    converged_warmth = wall_starting_warmth
    leftover_error = equation_source_term - apply_stiffness_matrix(
        converged_warmth, bordered_wall_warmth
    )
    scaled = leftover_error / diagonal

    def paired(residual_now, scaled_now, image_now):
        return lax.psum(
            (jnp.sum(residual_now * scaled_now), jnp.sum(scaled_now * image_now)), ("gx", "gy")
        )

    image = apply_stiffness_matrix(scaled, rimmed(scaled))
    inner_rz, curvature = paired(leftover_error, scaled, image)
    descent_length = inner_rz / curvature
    search_heading = scaled
    image_dir = image
    for iteration in range(ITERS):
        converged_warmth = converged_warmth + descent_length * search_heading
        leftover_error = leftover_error - descent_length * image_dir
        if iteration + 1 < ITERS:
            scaled = leftover_error / diagonal
            image = apply_stiffness_matrix(scaled, rimmed(scaled))
            inner_next, curvature = paired(leftover_error, scaled, image)
            ratio = inner_next / inner_rz
            descent_length = inner_next / (curvature - ratio * inner_next / descent_length)
            search_heading = scaled + ratio * search_heading
            image_dir = image + ratio * image_dir
            inner_rz = inner_next
    return (current_estimate, converged_warmth)


def solution(mesh):
    return jax.shard_map(
        local,
        mesh=mesh,
        in_specs=(
            P("gx", "gy", None),
            P("gx", "gy", None),
            P(None, "gx", "gy", None),
            P("gx", "gy", None),
            P("gx", "gy", None),
            P("gx", "gy", None),
            P("gx", "gy", None),
            P("gx", "gy", None),
            P("gx", "gy"),
        ),
        out_specs=(P("gx", "gy", None), P("gx", "gy", None)),
        check_vma=False,
    )
```

profile of v0, /device:TPU:0, one launch (start us, length us, event | category | flops | bytes accessed | tf_op | source)
XLA Modules:
  0.0 360.6 jit_solution(3652510717344675397)
XLA Ops:
  1.6 4.9 %collective-permute-start = (f32[1,16,1024]{2,1,0:T(8,128)S(1)}, f32[1,16,1024]{2,1,0:T(8,128)S(1)}, u32[]{:S(2)}, u32[]{:S(2)}) collective-permute-start(f32[1,16,1024]{2,1,0:T(8,128)S(1)} %get-tuple-element.112), channel_id=1, source_target_pairs={{0,4},{4,8},{8,12},{12,16},{16,20},{20,24},{24,28},{1,5},{5,9},{9,... | collective-permute-start | bytes 196616 | tf_op jit(solution)/shard_map/ppermute | solution.py:19
  6.5 1.4 collective-permute-start.1
  8.0 1.3 collective-permute-start.19
  9.3 5.2 %collective-permute-start.17 = (f32[1,16,1024]{2,1,0:T(8,128)S(1)}, f32[1,16,1024]{2,1,0:T(8,128)S(1)}, u32[]{:S(2)}, u32[]{:S(2)}) collective-permute-start(f32[1,16,1024]{2,1,0:T(8,128)S(1)} %get-tuple-element.91), channel_id=1, source_target_pairs={{0,4},{4,8},{8,12},{12,16},{16,20},{20,24},{24,28},{1,5},{5,9},{9,... | collective-permute-start | bytes 196616 | tf_op jit(solution)/shard_map/ppermute | solution.py:19
  14.5 4.8 %collective-permute-start.16 = (f32[1,16,1024]{2,1,0:T(8,128)S(1)}, f32[1,16,1024]{2,1,0:T(8,128)S(1)}, u32[]{:S(2)}, u32[]{:S(2)}) collective-permute-start(f32[1,16,1024]{2,1,0:T(8,128)S(1)} %get-tuple-element.96), channel_id=1, source_target_pairs={{0,4},{4,8},{8,12},{12,16},{16,20},{20,24},{24,28},{1,5},{5,9},{9,... | collective-permute-start | bytes 196616 | tf_op jit(solution)/shard_map/ppermute | solution.py:19
  22.1 5.3 %all-gather.1 = s32[4,16,4]{1,2,0:T(4,128)S(1)} all-gather(s32[1,16,4]{1,2,0:T(4,128)S(1)} %bitcast.80), channel_id=1, replica_groups=mesh['gx'=8,'gy'=4] {'gy'}, dimensions={0}, use_global_device_ids=true | all-gather | bytes 1280 | tf_op jit(solution)/shard_map/all_gather | solution.py:112
  27.6 5.4 %all-gather = f32[4,64,1]{2,1,0:T(8,128)S(1)} all-gather(f32[4,16,1]{2,1,0:T(8,128)S(1)} %slice.433), channel_id=2, replica_groups=mesh['gx'=8,'gy'=4] {'gy'}, dimensions={1}, use_global_device_ids=true | all-gather | bytes 1280 | tf_op jit(solution)/shard_map/all_gather | solution.py:86
  33.6 1.3 collective-permute-start.18
  34.9 4.9 %collective-permute-done.18 = f32[1,16,1024]{2,1,0:T(8,128)S(1)} collective-permute-done((f32[1,16,1024]{2,1,0:T(8,128)S(1)}, f32[1,16,1024]{2,1,0:T(8,128)S(1)}, u32[]{:S(2)}, u32[]{:S(2)}) %collective-permute-start.18) | collective-permute-done | bytes 65568 | tf_op jit(solution)/shard_map/ppermute | solution.py:21
  39.9 1.3 collective-permute-start.22
  41.2 3.0 collective-permute-start.20
  44.4 3.1 collective-permute-start.2
  47.6 1.3 collective-permute-start.3
  49.7 3.0 collective-permute-start.21
  53.2 4.3 %collective-permute-start.4 = (f32[1,16,1024]{2,1,0:T(8,128)S(1)}, f32[1,16,1024]{2,1,0:T(8,128)S(1)}, u32[]{:S(2)}, u32[]{:S(2)}) collective-permute-start(f32[1,16,1024]{2,1,0:T(8,128)S(1)} %get-tuple-element.108), channel_id=1, source_target_pairs={{0,4},{4,8},{8,12},{12,16},{16,20},{20,24},{24,28},{1,5},{5,9},{9,... | collective-permute-start | bytes 196616 | tf_op jit(solution)/shard_map/ppermute | solution.py:19
  57.5 1.3 collective-permute-start.5
  59.4 4.5 %collective-permute-done.5 = f32[1,16,1024]{2,1,0:T(8,128)S(1)} collective-permute-done((f32[1,16,1024]{2,1,0:T(8,128)S(1)}, f32[1,16,1024]{2,1,0:T(8,128)S(1)}, u32[]{:S(2)}, u32[]{:S(2)}) %collective-permute-start.5) | collective-permute-done | bytes 65568 | tf_op jit(solution)/shard_map/ppermute | solution.py:21
  63.9 2.2 collective-permute-start.6
  66.1 1.3 collective-permute-start.7
  67.5 2.4 collective-permute-done.7
  70.4 3.4 collective-permute-start.8
  73.8 1.3 collective-permute-start.9
  75.7 4.3 %collective-permute-done.9 = f32[1,16,1024]{2,1,0:T(8,128)S(1)} collective-permute-done((f32[1,16,1024]{2,1,0:T(8,128)S(1)}, f32[1,16,1024]{2,1,0:T(8,128)S(1)}, u32[]{:S(2)}, u32[]{:S(2)}) %collective-permute-start.9) | collective-permute-done | bytes 65568 | tf_op jit(solution)/shard_map/ppermute | solution.py:21
  80.0 3.0 collective-permute-start.10
  83.0 1.3 collective-permute-start.11
  84.4 1.3 collective-permute-start.23
  85.7 1.3 collective-permute-done.11
  87.6 6.6 %all-gather.2 = f32[4,16,4]{1,2,0:T(4,128)S(1)} all-gather(f32[1,16,4]{1,2,0:T(4,128)S(1)} %multiply_bitcast_fusion), channel_id=1, replica_groups=mesh['gx'=8,'gy'=4] {'gy'}, dimensions={0}, use_global_device_ids=true | all-gather | bytes 1280 | tf_op jit(solution)/shard_map/all_gather | solution.py:113
  95.7 2.8 fusion.162
  98.5 4.3 %collective-permute-start.24 = (f32[1,16,1024]{2,1,0:T(8,128)S(1)}, f32[1,16,1024]{2,1,0:T(8,128)S(1)}, u32[]{:S(2)}, u32[]{:S(2)}) collective-permute-start(f32[1,16,1024]{2,1,0:T(8,128)S(1)} %get-tuple-element.84), channel_id=1, source_target_pairs={{0,4},{4,8},{8,12},{12,16},{16,20},{20,24},{24,28},{1,5},{5,9},{9,... | collective-permute-start | bytes 196616 | tf_op jit(solution)/shard_map/ppermute | solution.py:19
  102.9 1.3 collective-permute-start.25
  105.0 4.0 %collective-permute-done.25 = f32[1,16,1024]{2,1,0:T(8,128)S(1)} collective-permute-done((f32[1,16,1024]{2,1,0:T(8,128)S(1)}, f32[1,16,1024]{2,1,0:T(8,128)S(1)}, u32[]{:S(2)}, u32[]{:S(2)}) %collective-permute-start.25) | collective-permute-done | bytes 65568 | tf_op jit(solution)/shard_map/ppermute | solution.py:21
  109.1 1.3 collective-permute-start.26
  110.4 1.3 collective-permute-start.27
  111.8 3.4 collective-permute-done.27
  115.3 1.7 multiply_reduce_fusion.5
  117.0 41.0 %all-reduce.19 = (f32[]{:T(128)}, f32[]{:T(128)}) all-reduce(f32[]{:T(128)} %get-tuple-element.27, f32[]{:T(128)} %get-tuple-element.26), channel_id=1, replica_groups=mesh['gx'=8,'gy'=4] {'gx','gy'}, use_global_device_ids=true, to_apply=%region_3.4 | all-reduce | flops 2 | bytes 16 | tf_op jit(solution)/shard_map/psum | solution.py:136
  160.4 4.4 %collective-permute-start.28 = (f32[1,16,1024]{2,1,0:T(8,128)S(1)}, f32[1,16,1024]{2,1,0:T(8,128)S(1)}, u32[]{:S(2)}, u32[]{:S(2)}) collective-permute-start(f32[1,16,1024]{2,1,0:T(8,128)S(1)} %get-tuple-element.80), channel_id=1, source_target_pairs={{0,4},{4,8},{8,12},{12,16},{16,20},{20,24},{24,28},{1,5},{5,9},{9,... | collective-permute-start | bytes 196616 | tf_op jit(solution)/shard_map/ppermute | solution.py:19
  164.8 1.3 collective-permute-start.29
  166.7 5.2 %collective-permute-start.12 = (f32[1,16,1024]{2,1,0:T(8,128)}, f32[1,16,1024]{2,1,0:T(8,128)}, u32[]{:S(2)}, u32[]{:S(2)}) collective-permute-start(f32[1,16,1024]{2,1,0:T(8,128)} %get-tuple-element.100), channel_id=1, source_target_pairs={{0,4},{4,8},{8,12},{12,16},{16,20},{20,24},{24,28},{1,5},{5,9},{9,... | collective-permute-start | bytes 196616 | tf_op jit(solution)/shard_map/ppermute | solution.py:19
  171.9 1.3 collective-permute-start.13
  173.3 1.3 collective-permute-start.30
  174.6 1.4 collective-permute-start.31
  176.1 2.9 collective-permute-done.31
  179.1 1.7 multiply_reduce_fusion.3
  180.8 42.0 %all-reduce.18 = (f32[]{:T(128)}, f32[]{:T(128)}) all-reduce(f32[]{:T(128)} %get-tuple-element.25, f32[]{:T(128)} %get-tuple-element.24), channel_id=1, replica_groups=mesh['gx'=8,'gy'=4] {'gx','gy'}, use_global_device_ids=true, to_apply=%region_7.8 | all-reduce | flops 2 | bytes 16 | tf_op jit(solution)/shard_map/psum | solution.py:136
  228.3 4.4 %collective-permute-start.32 = (f32[1,16,1024]{2,1,0:T(8,128)S(1)}, f32[1,16,1024]{2,1,0:T(8,128)S(1)}, u32[]{:S(2)}, u32[]{:S(2)}) collective-permute-start(f32[1,16,1024]{2,1,0:T(8,128)S(1)} %get-tuple-element.76), channel_id=1, source_target_pairs={{0,4},{4,8},{8,12},{12,16},{16,20},{20,24},{24,28},{1,5},{5,9},{9,... | collective-permute-start | bytes 196616 | tf_op jit(solution)/shard_map/ppermute | solution.py:19
  232.7 1.3 collective-permute-start.33
  234.0 1.5 pad_maximum_fusion.86
  235.5 1.9 collective-permute-start.14
  238.9 4.5 %collective-permute-start.34 = (f32[6,1,1024]{2,1,0:T(1,128)S(1)}, f32[6,1,1024]{2,1,0:T(1,128)S(1)}, u32[]{:S(2)}, u32[]{:S(2)}) collective-permute-start(f32[6,1,1024]{2,1,0:T(1,128)S(1)} %get-tuple-element.54), channel_id=1, source_target_pairs={{0,1},{1,2},{2,3},{4,5},{5,6},{6,7},{8,9},{9,10},{10,11},{12,13},{... | collective-permute-start | bytes 73736 | tf_op jit(solution)/shard_map/ppermute | solution.py:19
  243.4 1.4 collective-permute-start.35
  245.0 2.9 collective-permute-done.35
  247.9 1.7 multiply_reduce_fusion.1
  249.6 41.4 %all-reduce.17 = (f32[]{:T(128)}, f32[]{:T(128)}) all-reduce(f32[]{:T(128)} %get-tuple-element.23, f32[]{:T(128)} %get-tuple-element.22), channel_id=1, replica_groups=mesh['gx'=8,'gy'=4] {'gx','gy'}, use_global_device_ids=true, to_apply=%region_11.12 | all-reduce | flops 2 | bytes 16 | tf_op jit(solution)/shard_map/psum | solution.py:136
  294.8 2.0 multiply_reduce_fusion
  296.8 4.6 %collective-permute-start.36 = (f32[1,16,1024]{2,1,0:T(8,128)S(1)}, f32[1,16,1024]{2,1,0:T(8,128)S(1)}, u32[]{:S(2)}, u32[]{:S(2)}) collective-permute-start(f32[1,16,1024]{2,1,0:T(8,128)S(1)} %get-tuple-element.74), channel_id=1, source_target_pairs={{0,4},{4,8},{8,12},{12,16},{16,20},{20,24},{24,28},{1,5},{5,9},{9,... | collective-permute-start | bytes 196616 | tf_op jit(solution)/shard_map/ppermute | solution.py:19
  301.4 1.3 collective-permute-start.37
  302.8 2.0 fusion.91
  304.7 2.8 collective-permute-done.37
  307.6 1.3 collective-permute-start.38
  308.9 1.4 collective-permute-start.39
  310.5 3.3 collective-permute-done.39
  314.8 41.4 %all-reduce.16 = (f32[]{:T(128)}, f32[]{:T(128)}) all-reduce(f32[]{:T(128)} %get-tuple-element.36, f32[]{:T(128)} %fusion.6), channel_id=1, replica_groups=mesh['gx'=8,'gy'=4] {'gx','gy'}, use_global_device_ids=true, to_apply=%region_15.16 | all-reduce | flops 2 | bytes 16 | tf_op jit(solution)/shard_map/psum | solution.py:136
  (167 shorter events, 17.4 us)
Async XLA Ops:
  0.6 7.3 %copy-start.3 = (f32[4,16,1024]{2,1,0:T(8,128)S(1)}, f32[4,16,1024]{2,1,0:T(8,128)}, u32[]{:S(2)}) copy-start(f32[4,16,1024]{2,1,0:T(8,128)} %param.15) | copy-start | bytes 786436
  0.6 13.8 %copy-start = (f32[4,16,1024]{2,1,0:T(8,128)S(1)}, f32[4,16,1024]{2,1,0:T(8,128)}, u32[]{:S(2)}) copy-start(f32[4,16,1024]{2,1,0:T(8,128)} %param.17) | copy-start | bytes 786436
  1.6 39.6 %collective-permute-start = (f32[1,16,1024]{2,1,0:T(8,128)S(1)}, f32[1,16,1024]{2,1,0:T(8,128)S(1)}, u32[]{:S(2)}, u32[]{:S(2)}) collective-permute-start(f32[1,16,1024]{2,1,0:T(8,128)S(1)} %get-tuple-element.112), channel_id=1, source_target_pairs={{0,4},{4,8},{8,12},{12,16},{16,20},{20,24},{24,28},{1,5},{5,9},{9,... | collective-permute-start | bytes 196616 | tf_op jit(solution)/shard_map/ppermute | solution.py:19
  6.5 12.8 %copy-start.13 = (f32[4,16,1024]{2,1,0:T(8,128)S(1)}, f32[4,16,1024]{2,1,0:T(8,128)}, u32[]{:S(2)}) copy-start(f32[4,16,1024]{2,1,0:T(8,128)} %param.11) | copy-start | bytes 786436
  6.5 37.8 %collective-permute-start.1 = (f32[1,16,1024]{2,1,0:T(8,128)S(1)}, f32[1,16,1024]{2,1,0:T(8,128)S(1)}, u32[]{:S(2)}, u32[]{:S(2)}) collective-permute-start(f32[1,16,1024]{2,1,0:T(8,128)S(1)} %get-tuple-element.113), channel_id=1, source_target_pairs={{4,0},{8,4},{12,8},{16,12},{20,16},{24,20},{28,24},{5,1},{9,5},{13... | collective-permute-start | bytes 196616 | tf_op jit(solution)/shard_map/ppermute | solution.py:21
  8.0 41.0 %collective-permute-start.19 = (f32[1,16,1024]{2,1,0:T(8,128)S(1)}, f32[1,16,1024]{2,1,0:T(8,128)S(1)}, u32[]{:S(2)}, u32[]{:S(2)}) collective-permute-start(f32[1,16,1024]{2,1,0:T(8,128)S(1)} %get-tuple-element.90), channel_id=1, source_target_pairs={{4,0},{8,4},{12,8},{16,12},{20,16},{24,20},{28,24},{5,1},{9,5},{13... | collective-permute-start | bytes 196616 | tf_op jit(solution)/shard_map/ppermute | solution.py:21
  9.3 38.3 %collective-permute-start.17 = (f32[1,16,1024]{2,1,0:T(8,128)S(1)}, f32[1,16,1024]{2,1,0:T(8,128)S(1)}, u32[]{:S(2)}, u32[]{:S(2)}) collective-permute-start(f32[1,16,1024]{2,1,0:T(8,128)S(1)} %get-tuple-element.91), channel_id=1, source_target_pairs={{0,4},{4,8},{8,12},{12,16},{16,20},{20,24},{24,28},{1,5},{5,9},{9,... | collective-permute-start | bytes 196616 | tf_op jit(solution)/shard_map/ppermute | solution.py:19
  14.5 19.1 %collective-permute-start.16 = (f32[1,16,1024]{2,1,0:T(8,128)S(1)}, f32[1,16,1024]{2,1,0:T(8,128)S(1)}, u32[]{:S(2)}, u32[]{:S(2)}) collective-permute-start(f32[1,16,1024]{2,1,0:T(8,128)S(1)} %get-tuple-element.96), channel_id=1, source_target_pairs={{0,4},{4,8},{8,12},{12,16},{16,20},{20,24},{24,28},{1,5},{5,9},{9,... | collective-permute-start | bytes 196616 | tf_op jit(solution)/shard_map/ppermute | solution.py:19
  22.1 5.4 %copy-start.33 = (s32[4,16,8]{1,2,0:T(8,128)S(1)}, s32[4,16,8]{1,2,0:T(8,128)}, u32[]{:S(2)}) copy-start(s32[4,16,8]{1,2,0:T(8,128)} %param.14) | copy-start | bytes 6148
  33.4 53.7 %copy-start.22 = (f32[4,16,1]{2,1,0:T(8,128)}, f32[4,16,1]{2,1,0:T(8,128)S(1)}, u32[]{:S(2)}) copy-start(f32[4,16,1]{2,1,0:T(8,128)S(1)} %copy.374) | copy-start | bytes 772
  33.6 6.2 %collective-permute-start.18 = (f32[1,16,1024]{2,1,0:T(8,128)S(1)}, f32[1,16,1024]{2,1,0:T(8,128)S(1)}, u32[]{:S(2)}, u32[]{:S(2)}) collective-permute-start(f32[1,16,1024]{2,1,0:T(8,128)S(1)} %get-tuple-element.97), channel_id=1, source_target_pairs={{4,0},{8,4},{12,8},{16,12},{20,16},{24,20},{28,24},{5,1},{9,5},{13... | collective-permute-start | bytes 196616 | tf_op jit(solution)/shard_map/ppermute | solution.py:21
  39.8 4.5 %copy-start.25 = (f32[6,16,1024]{2,1,0:T(8,128)}, f32[6,16,1024]{2,1,0:T(8,128)S(1)}, u32[]{:S(2)}) copy-start(f32[6,16,1024]{2,1,0:T(8,128)S(1)} %constant_dynamic-update-slice_fusion.3) | copy-start | bytes 1179652
  39.9 55.1 %collective-permute-start.22 = (f32[6,1,1024]{2,1,0:T(1,128)S(1)}, f32[6,1,1024]{2,1,0:T(1,128)S(1)}, u32[]{:S(2)}, u32[]{:S(2)}) collective-permute-start(f32[6,1,1024]{2,1,0:T(1,128)S(1)} %get-tuple-element.60), channel_id=1, source_target_pairs={{1,0},{2,1},{3,2},{5,4},{6,5},{7,6},{9,8},{10,9},{11,10},{13,12},{... | collective-permute-start | bytes 73736 | tf_op jit(solution)/shard_map/ppermute | solution.py:21
  41.2 53.8 %collective-permute-start.20 = (f32[6,1,1024]{2,1,0:T(1,128)S(1)}, f32[6,1,1024]{2,1,0:T(1,128)S(1)}, u32[]{:S(2)}, u32[]{:S(2)}) collective-permute-start(f32[6,1,1024]{2,1,0:T(1,128)S(1)} %get-tuple-element.61), channel_id=1, source_target_pairs={{0,1},{1,2},{2,3},{4,5},{5,6},{6,7},{8,9},{9,10},{10,11},{12,13},{... | collective-permute-start | bytes 73736 | tf_op jit(solution)/shard_map/ppermute | solution.py:19
  44.3 4.6 %copy-start.28 = (f32[4,16,1024]{2,1,0:T(8,128)S(1)}, f32[4,16,1024]{2,1,0:T(8,128)}, u32[]{:S(2)}) copy-start(f32[4,16,1024]{2,1,0:T(8,128)} %param.18) | copy-start | bytes 786436
  44.3 4.6 %copy-start.2 = (f32[4,16,1024]{2,1,0:T(8,128)S(1)}, f32[4,16,1024]{2,1,0:T(8,128)}, u32[]{:S(2)}) copy-start(f32[4,16,1024]{2,1,0:T(8,128)} %param.16) | copy-start | bytes 786436
  44.4 8.3 %collective-permute-start.2 = (f32[6,1,1024]{2,1,0:T(1,128)S(1)}, f32[6,1,1024]{2,1,0:T(1,128)S(1)}, u32[]{:S(2)}, u32[]{:S(2)}) collective-permute-start(f32[6,1,1024]{2,1,0:T(1,128)S(1)} %get-tuple-element.70), channel_id=1, source_target_pairs={{0,1},{1,2},{2,3},{4,5},{5,6},{6,7},{8,9},{9,10},{10,11},{12,13},{... | collective-permute-start | bytes 73736 | tf_op jit(solution)/shard_map/ppermute | solution.py:19
  47.6 5.2 %collective-permute-start.3 = (f32[6,1,1024]{2,1,0:T(1,128)S(1)}, f32[6,1,1024]{2,1,0:T(1,128)S(1)}, u32[]{:S(2)}, u32[]{:S(2)}) collective-permute-start(f32[6,1,1024]{2,1,0:T(1,128)S(1)} %get-tuple-element.71), channel_id=1, source_target_pairs={{1,0},{2,1},{3,2},{5,4},{6,5},{7,6},{9,8},{10,9},{11,10},{13,12},{... | collective-permute-start | bytes 73736 | tf_op jit(solution)/shard_map/ppermute | solution.py:21
  49.7 45.4 %collective-permute-start.21 = (f32[6,1,1024]{2,1,0:T(1,128)S(1)}, f32[6,1,1024]{2,1,0:T(1,128)S(1)}, u32[]{:S(2)}, u32[]{:S(2)}) collective-permute-start(f32[6,1,1024]{2,1,0:T(1,128)S(1)} %get-tuple-element.62), channel_id=1, source_target_pairs={{0,1},{1,2},{2,3},{4,5},{5,6},{6,7},{8,9},{9,10},{10,11},{12,13},{... | collective-permute-start | bytes 73736 | tf_op jit(solution)/shard_map/ppermute | solution.py:19
  53.2 6.2 %collective-permute-start.4 = (f32[1,16,1024]{2,1,0:T(8,128)S(1)}, f32[1,16,1024]{2,1,0:T(8,128)S(1)}, u32[]{:S(2)}, u32[]{:S(2)}) collective-permute-start(f32[1,16,1024]{2,1,0:T(8,128)S(1)} %get-tuple-element.108), channel_id=1, source_target_pairs={{0,4},{4,8},{8,12},{12,16},{16,20},{20,24},{24,28},{1,5},{5,9},{9,... | collective-permute-start | bytes 196616 | tf_op jit(solution)/shard_map/ppermute | solution.py:19
  57.5 6.4 %collective-permute-start.5 = (f32[1,16,1024]{2,1,0:T(8,128)S(1)}, f32[1,16,1024]{2,1,0:T(8,128)S(1)}, u32[]{:S(2)}, u32[]{:S(2)}) collective-permute-start(f32[1,16,1024]{2,1,0:T(8,128)S(1)} %get-tuple-element.109), channel_id=1, source_target_pairs={{4,0},{8,4},{12,8},{16,12},{20,16},{24,20},{28,24},{5,1},{9,5},{13... | collective-permute-start | bytes 196616 | tf_op jit(solution)/shard_map/ppermute | solution.py:21
  63.9 3.6 %collective-permute-start.6 = (f32[6,1,1024]{2,1,0:T(1,128)S(1)}, f32[6,1,1024]{2,1,0:T(1,128)S(1)}, u32[]{:S(2)}, u32[]{:S(2)}) collective-permute-start(f32[6,1,1024]{2,1,0:T(1,128)S(1)} %get-tuple-element.68), channel_id=1, source_target_pairs={{0,1},{1,2},{2,3},{4,5},{5,6},{6,7},{8,9},{9,10},{10,11},{12,13},{... | collective-permute-start | bytes 73736 | tf_op jit(solution)/shard_map/ppermute | solution.py:19
  66.1 3.8 %collective-permute-start.7 = (f32[6,1,1024]{2,1,0:T(1,128)S(1)}, f32[6,1,1024]{2,1,0:T(1,128)S(1)}, u32[]{:S(2)}, u32[]{:S(2)}) collective-permute-start(f32[6,1,1024]{2,1,0:T(1,128)S(1)} %get-tuple-element.69), channel_id=1, source_target_pairs={{1,0},{2,1},{3,2},{5,4},{6,5},{7,6},{9,8},{10,9},{11,10},{13,12},{... | collective-permute-start | bytes 73736 | tf_op jit(solution)/shard_map/ppermute | solution.py:21
  70.4 5.3 %collective-permute-start.8 = (f32[1,16,1024]{2,1,0:T(8,128)S(1)}, f32[1,16,1024]{2,1,0:T(8,128)S(1)}, u32[]{:S(2)}, u32[]{:S(2)}) collective-permute-start(f32[1,16,1024]{2,1,0:T(8,128)S(1)} %get-tuple-element.104), channel_id=1, source_target_pairs={{0,4},{4,8},{8,12},{12,16},{16,20},{20,24},{24,28},{1,5},{5,9},{9,... | collective-permute-start | bytes 196616 | tf_op jit(solution)/shard_map/ppermute | solution.py:19
  73.8 6.2 %collective-permute-start.9 = (f32[1,16,1024]{2,1,0:T(8,128)S(1)}, f32[1,16,1024]{2,1,0:T(8,128)S(1)}, u32[]{:S(2)}, u32[]{:S(2)}) collective-permute-start(f32[1,16,1024]{2,1,0:T(8,128)S(1)} %get-tuple-element.105), channel_id=1, source_target_pairs={{4,0},{8,4},{12,8},{16,12},{20,16},{24,20},{28,24},{5,1},{9,5},{13... | collective-permute-start | bytes 196616 | tf_op jit(solution)/shard_map/ppermute | solution.py:21
  80.0 4.4 %collective-permute-start.10 = (f32[6,1,1024]{2,1,0:T(1,128)S(1)}, f32[6,1,1024]{2,1,0:T(1,128)S(1)}, u32[]{:S(2)}, u32[]{:S(2)}) collective-permute-start(f32[6,1,1024]{2,1,0:T(1,128)S(1)} %get-tuple-element.66), channel_id=1, source_target_pairs={{0,1},{1,2},{2,3},{4,5},{5,6},{6,7},{8,9},{9,10},{10,11},{12,13},{... | collective-permute-start | bytes 73736 | tf_op jit(solution)/shard_map/ppermute | solution.py:19
  83.0 4.0 %collective-permute-start.11 = (f32[6,1,1024]{2,1,0:T(1,128)S(1)}, f32[6,1,1024]{2,1,0:T(1,128)S(1)}, u32[]{:S(2)}, u32[]{:S(2)}) collective-permute-start(f32[6,1,1024]{2,1,0:T(1,128)S(1)} %get-tuple-element.67), channel_id=1, source_target_pairs={{1,0},{2,1},{3,2},{5,4},{6,5},{7,6},{9,8},{10,9},{11,10},{13,12},{... | collective-permute-start | bytes 73736 | tf_op jit(solution)/shard_map/ppermute | solution.py:21
  84.4 10.6 %collective-permute-start.23 = (f32[6,1,1024]{2,1,0:T(1,128)S(1)}, f32[6,1,1024]{2,1,0:T(1,128)S(1)}, u32[]{:S(2)}, u32[]{:S(2)}) collective-permute-start(f32[6,1,1024]{2,1,0:T(1,128)S(1)} %get-tuple-element.63), channel_id=1, source_target_pairs={{1,0},{2,1},{3,2},{5,4},{6,5},{7,6},{9,8},{10,9},{11,10},{13,12},{... | collective-permute-start | bytes 73736 | tf_op jit(solution)/shard_map/ppermute | solution.py:21
  98.5 16.8 %copy-start.9 = (f32[4,16,1024]{2,1,0:T(8,128)}, f32[4,16,1024]{2,1,0:T(8,128)S(1)}, u32[]{:S(2)}) copy-start(f32[4,16,1024]{2,1,0:T(8,128)S(1)} %get-tuple-element.51) | copy-start | bytes 786436
  98.5 16.8 %copy-start.16 = (f32[4,16,1024]{2,1,0:T(8,128)}, f32[4,16,1024]{2,1,0:T(8,128)S(1)}, u32[]{:S(2)}) copy-start(f32[4,16,1024]{2,1,0:T(8,128)S(1)} %get-tuple-element.47) | copy-start | bytes 786436
  98.5 80.6 %copy-start.6 = (f32[4,16,1024]{2,1,0:T(8,128)}, f32[4,16,1024]{2,1,0:T(8,128)S(1)}, u32[]{:S(2)}) copy-start(f32[4,16,1024]{2,1,0:T(8,128)S(1)} %get-tuple-element.50) | copy-start | bytes 786436
  98.5 149.3 %copy-start.4 = (f32[4,16,1024]{2,1,0:T(8,128)}, f32[4,16,1024]{2,1,0:T(8,128)S(1)}, u32[]{:S(2)}) copy-start(f32[4,16,1024]{2,1,0:T(8,128)S(1)} %get-tuple-element.49) | copy-start | bytes 786436
  98.5 6.5 %collective-permute-start.24 = (f32[1,16,1024]{2,1,0:T(8,128)S(1)}, f32[1,16,1024]{2,1,0:T(8,128)S(1)}, u32[]{:S(2)}, u32[]{:S(2)}) collective-permute-start(f32[1,16,1024]{2,1,0:T(8,128)S(1)} %get-tuple-element.84), channel_id=1, source_target_pairs={{0,4},{4,8},{8,12},{12,16},{16,20},{20,24},{24,28},{1,5},{5,9},{9,... | collective-permute-start | bytes 196616 | tf_op jit(solution)/shard_map/ppermute | solution.py:19
  102.9 6.2 %collective-permute-start.25 = (f32[1,16,1024]{2,1,0:T(8,128)S(1)}, f32[1,16,1024]{2,1,0:T(8,128)S(1)}, u32[]{:S(2)}, u32[]{:S(2)}) collective-permute-start(f32[1,16,1024]{2,1,0:T(8,128)S(1)} %get-tuple-element.85), channel_id=1, source_target_pairs={{4,0},{8,4},{12,8},{16,12},{20,16},{24,20},{28,24},{5,1},{9,5},{13... | collective-permute-start | bytes 196616 | tf_op jit(solution)/shard_map/ppermute | solution.py:21
  109.1 2.7 collective-permute-start.26
  110.4 4.9 %collective-permute-start.27 = (f32[6,1,1024]{2,1,0:T(1,128)S(1)}, f32[6,1,1024]{2,1,0:T(1,128)S(1)}, u32[]{:S(2)}, u32[]{:S(2)}) collective-permute-start(f32[6,1,1024]{2,1,0:T(1,128)S(1)} %get-tuple-element.59), channel_id=1, source_target_pairs={{1,0},{2,1},{3,2},{5,4},{6,5},{7,6},{9,8},{10,9},{11,10},{13,12},{... | collective-permute-start | bytes 73736 | tf_op jit(solution)/shard_map/ppermute | solution.py:21
  160.4 18.7 %copy-start.17 = (f32[4,16,1024]{2,1,0:T(8,128)}, f32[4,16,1024]{2,1,0:T(8,128)S(1)}, u32[]{:S(2)}) copy-start(f32[4,16,1024]{2,1,0:T(8,128)S(1)} %get-tuple-element.43) | copy-start | bytes 786436
  160.4 12.8 %collective-permute-start.28 = (f32[1,16,1024]{2,1,0:T(8,128)S(1)}, f32[1,16,1024]{2,1,0:T(8,128)S(1)}, u32[]{:S(2)}, u32[]{:S(2)}) collective-permute-start(f32[1,16,1024]{2,1,0:T(8,128)S(1)} %get-tuple-element.80), channel_id=1, source_target_pairs={{0,4},{4,8},{8,12},{12,16},{16,20},{20,24},{24,28},{1,5},{5,9},{9,... | collective-permute-start | bytes 196616 | tf_op jit(solution)/shard_map/ppermute | solution.py:19
  164.8 8.4 %collective-permute-start.29 = (f32[1,16,1024]{2,1,0:T(8,128)S(1)}, f32[1,16,1024]{2,1,0:T(8,128)S(1)}, u32[]{:S(2)}, u32[]{:S(2)}) collective-permute-start(f32[1,16,1024]{2,1,0:T(8,128)S(1)} %get-tuple-element.81), channel_id=1, source_target_pairs={{4,0},{8,4},{12,8},{16,12},{20,16},{24,20},{28,24},{5,1},{9,5},{13... | collective-permute-start | bytes 196616 | tf_op jit(solution)/shard_map/ppermute | solution.py:21
  166.7 67.2 %collective-permute-start.12 = (f32[1,16,1024]{2,1,0:T(8,128)}, f32[1,16,1024]{2,1,0:T(8,128)}, u32[]{:S(2)}, u32[]{:S(2)}) collective-permute-start(f32[1,16,1024]{2,1,0:T(8,128)} %get-tuple-element.100), channel_id=1, source_target_pairs={{0,4},{4,8},{8,12},{12,16},{16,20},{20,24},{24,28},{1,5},{5,9},{9,... | collective-permute-start | bytes 196616 | tf_op jit(solution)/shard_map/ppermute | solution.py:19
  171.9 62.1 %collective-permute-start.13 = (f32[1,16,1024]{2,1,0:T(8,128)}, f32[1,16,1024]{2,1,0:T(8,128)}, u32[]{:S(2)}, u32[]{:S(2)}) collective-permute-start(f32[1,16,1024]{2,1,0:T(8,128)} %get-tuple-element.101), channel_id=1, source_target_pairs={{4,0},{8,4},{12,8},{16,12},{20,16},{24,20},{28,24},{5,1},{9,5},{13... | collective-permute-start | bytes 196616 | tf_op jit(solution)/shard_map/ppermute | solution.py:21
  173.3 2.9 collective-permute-start.30
  174.6 4.5 %copy-start.10 = (f32[4,16,1024]{2,1,0:T(8,128)S(1)}, f32[4,16,1024]{2,1,0:T(8,128)}, u32[]{:S(2)}) copy-start(f32[4,16,1024]{2,1,0:T(8,128)} %copy-done.9) | copy-start | bytes 786436
  174.6 4.5 %collective-permute-start.31 = (f32[6,1,1024]{2,1,0:T(1,128)S(1)}, f32[6,1,1024]{2,1,0:T(1,128)S(1)}, u32[]{:S(2)}, u32[]{:S(2)}) collective-permute-start(f32[6,1,1024]{2,1,0:T(1,128)S(1)} %get-tuple-element.57), channel_id=1, source_target_pairs={{1,0},{2,1},{3,2},{5,4},{6,5},{7,6},{9,8},{10,9},{11,10},{13,12},{... | collective-permute-start | bytes 73736 | tf_op jit(solution)/shard_map/ppermute | solution.py:21
  228.2 19.6 %copy-start.18 = (f32[4,16,1024]{2,1,0:T(8,128)}, f32[4,16,1024]{2,1,0:T(8,128)S(1)}, u32[]{:S(2)}) copy-start(f32[4,16,1024]{2,1,0:T(8,128)S(1)} %get-tuple-element.40) | copy-start | bytes 786436
  228.3 10.4 %collective-permute-start.32 = (f32[1,16,1024]{2,1,0:T(8,128)S(1)}, f32[1,16,1024]{2,1,0:T(8,128)S(1)}, u32[]{:S(2)}, u32[]{:S(2)}) collective-permute-start(f32[1,16,1024]{2,1,0:T(8,128)S(1)} %get-tuple-element.76), channel_id=1, source_target_pairs={{0,4},{4,8},{8,12},{12,16},{16,20},{20,24},{24,28},{1,5},{5,9},{9,... | collective-permute-start | bytes 196616 | tf_op jit(solution)/shard_map/ppermute | solution.py:19
  232.7 6.2 %collective-permute-start.33 = (f32[1,16,1024]{2,1,0:T(8,128)S(1)}, f32[1,16,1024]{2,1,0:T(8,128)S(1)}, u32[]{:S(2)}, u32[]{:S(2)}) collective-permute-start(f32[1,16,1024]{2,1,0:T(8,128)S(1)} %get-tuple-element.77), channel_id=1, source_target_pairs={{4,0},{8,4},{12,8},{16,12},{20,16},{24,20},{28,24},{5,1},{9,5},{13... | collective-permute-start | bytes 196616 | tf_op jit(solution)/shard_map/ppermute | solution.py:21
  235.5 67.2 %collective-permute-start.14 = (f32[6,1,1024]{2,1,0:T(1,128)}, f32[6,1,1024]{2,1,0:T(1,128)}, u32[]{:S(2)}, u32[]{:S(2)}) collective-permute-start(f32[6,1,1024]{2,1,0:T(1,128)} %get-tuple-element.64), channel_id=1, source_target_pairs={{0,1},{1,2},{2,3},{4,5},{5,6},{6,7},{8,9},{9,10},{10,11},{12,13},{... | collective-permute-start | bytes 73736 | tf_op jit(solution)/shard_map/ppermute | solution.py:19
  237.3 65.4 %collective-permute-start.15 = (f32[6,1,1024]{2,1,0:T(1,128)}, f32[6,1,1024]{2,1,0:T(1,128)}, u32[]{:S(2)}, u32[]{:S(2)}) collective-permute-start(f32[6,1,1024]{2,1,0:T(1,128)} %get-tuple-element.65), channel_id=1, source_target_pairs={{1,0},{2,1},{3,2},{5,4},{6,5},{7,6},{9,8},{10,9},{11,10},{13,12},{... | collective-permute-start | bytes 73736 | tf_op jit(solution)/shard_map/ppermute | solution.py:21
  238.9 6.1 %collective-permute-start.34 = (f32[6,1,1024]{2,1,0:T(1,128)S(1)}, f32[6,1,1024]{2,1,0:T(1,128)S(1)}, u32[]{:S(2)}, u32[]{:S(2)}) collective-permute-start(f32[6,1,1024]{2,1,0:T(1,128)S(1)} %get-tuple-element.54), channel_id=1, source_target_pairs={{0,1},{1,2},{2,3},{4,5},{5,6},{6,7},{8,9},{9,10},{10,11},{12,13},{... | collective-permute-start | bytes 73736 | tf_op jit(solution)/shard_map/ppermute | solution.py:19
  243.4 4.5 %copy-start.7 = (f32[4,16,1024]{2,1,0:T(8,128)S(1)}, f32[4,16,1024]{2,1,0:T(8,128)}, u32[]{:S(2)}) copy-start(f32[4,16,1024]{2,1,0:T(8,128)} %copy-done.6) | copy-start | bytes 786436
  243.4 4.5 %copy-start.11 = (f32[4,16,1024]{2,1,0:T(8,128)S(1)}, f32[4,16,1024]{2,1,0:T(8,128)}, u32[]{:S(2)}) copy-start(f32[4,16,1024]{2,1,0:T(8,128)} %copy-done.9) | copy-start | bytes 786436
  243.4 4.5 %collective-permute-start.35 = (f32[6,1,1024]{2,1,0:T(1,128)S(1)}, f32[6,1,1024]{2,1,0:T(1,128)S(1)}, u32[]{:S(2)}, u32[]{:S(2)}) collective-permute-start(f32[6,1,1024]{2,1,0:T(1,128)S(1)} %get-tuple-element.55), channel_id=1, source_target_pairs={{1,0},{2,1},{3,2},{5,4},{6,5},{7,6},{9,8},{10,9},{11,10},{13,12},{... | collective-permute-start | bytes 73736 | tf_op jit(solution)/shard_map/ppermute | solution.py:21
  294.7 8.0 %copy-start.20 = (f32[4,16,1023]{2,1,0:T(8,128)S(1)}, f32[4,16,1023]{2,1,0:T(8,128)}, u32[]{:S(2)}) copy-start(f32[4,16,1023]{2,1,0:T(8,128)} %get-tuple-element.98) | copy-start | bytes 785668
  294.8 8.0 %copy-start.21 = (f32[4,16,1023]{2,1,0:T(8,128)S(1)}, f32[4,16,1023]{2,1,0:T(8,128)}, u32[]{:S(2)}) copy-start(f32[4,16,1023]{2,1,0:T(8,128)} %get-tuple-element.99) | copy-start | bytes 785668
  294.8 8.0 %copy-start.23 = (f32[4,16,1]{2,1,0:T(8,128)S(1)}, f32[4,16,1]{2,1,0:T(8,128)}, u32[]{:S(2)}) copy-start(f32[4,16,1]{2,1,0:T(8,128)} %copy-done.22) | copy-start | bytes 772
  296.8 5.9 %copy-start.15 = (f32[4,16,1024]{2,1,0:T(8,128)S(1)}, f32[4,16,1024]{2,1,0:T(8,128)}, u32[]{:S(2)}) copy-start(f32[4,16,1024]{2,1,0:T(8,128)} %param.12) | copy-start | bytes 786436
  296.8 7.9 %collective-permute-start.36 = (f32[1,16,1024]{2,1,0:T(8,128)S(1)}, f32[1,16,1024]{2,1,0:T(8,128)S(1)}, u32[]{:S(2)}, u32[]{:S(2)}) collective-permute-start(f32[1,16,1024]{2,1,0:T(8,128)S(1)} %get-tuple-element.74), channel_id=1, source_target_pairs={{0,4},{4,8},{8,12},{12,16},{16,20},{20,24},{24,28},{1,5},{5,9},{9,... | collective-permute-start | bytes 196616 | tf_op jit(solution)/shard_map/ppermute | solution.py:19
  301.4 6.2 %collective-permute-start.37 = (f32[1,16,1024]{2,1,0:T(8,128)S(1)}, f32[1,16,1024]{2,1,0:T(8,128)S(1)}, u32[]{:S(2)}, u32[]{:S(2)}) collective-permute-start(f32[1,16,1024]{2,1,0:T(8,128)S(1)} %get-tuple-element.75), channel_id=1, source_target_pairs={{4,0},{8,4},{12,8},{16,12},{20,16},{24,20},{28,24},{5,1},{9,5},{13... | collective-permute-start | bytes 196616 | tf_op jit(solution)/shard_map/ppermute | solution.py:21
  307.6 2.9 collective-permute-start.38
  308.9 5.0 %copy-start.5 = (f32[4,16,1024]{2,1,0:T(8,128)S(1)}, f32[4,16,1024]{2,1,0:T(8,128)}, u32[]{:S(2)}) copy-start(f32[4,16,1024]{2,1,0:T(8,128)} %copy-done.4) | copy-start | bytes 786436
  308.9 4.9 %copy-start.8 = (f32[4,16,1024]{2,1,0:T(8,128)S(1)}, f32[4,16,1024]{2,1,0:T(8,128)}, u32[]{:S(2)}) copy-start(f32[4,16,1024]{2,1,0:T(8,128)} %copy-done.6) | copy-start | bytes 786436
  308.9 4.9 %copy-start.12 = (f32[4,16,1024]{2,1,0:T(8,128)S(1)}, f32[4,16,1024]{2,1,0:T(8,128)}, u32[]{:S(2)}) copy-start(f32[4,16,1024]{2,1,0:T(8,128)} %copy-done.9) | copy-start | bytes 786436
  308.9 4.9 %collective-permute-start.39 = (f32[6,1,1024]{2,1,0:T(1,128)S(1)}, f32[6,1,1024]{2,1,0:T(1,128)S(1)}, u32[]{:S(2)}, u32[]{:S(2)}) collective-permute-start(f32[6,1,1024]{2,1,0:T(1,128)S(1)} %get-tuple-element.53), channel_id=1, source_target_pairs={{1,0},{2,1},{3,2},{5,4},{6,5},{7,6},{9,8},{10,9},{11,10},{13,12},{... | collective-permute-start | bytes 73736 | tf_op jit(solution)/shard_map/ppermute | solution.py:21
  (11 other events, 16.7 us)
where the time goes:
time: 363 us; the launch traced here: 361 us
  blocking collectives  183 us (50%)
  starting transfers between devices  96.6 us (27%)
  waiting for transfers between devices  38 us (10%)
  other arithmetic  19.5 us (5%)
  between operations  14.5 us (4%)
  local copies, waits for them, and re-layouts  8.88 us (2%)
    psum x4, blocking collectives, paired(): lax.psum((jnp.sum(residual_now * scaled_now), jnp.sum(scaled_now * image_...  166 us
    ppermute x20, starting transfers between devices, padded_2(): lax.ppermute(tail, axis, [(i, (i + 1) % count) for i in range(ends)])  70.2 us
    ppermute x20, waiting for transfers between devices, padded_2(): lax.ppermute(head, axis, [((i + 1) % count, i) for i in range(ends)])  37.1 us
    ppermute x20, starting transfers between devices, padded_2(): lax.ppermute(head, axis, [((i + 1) % count, i) for i in range(ends)])  26.3 us
  transfers between devices with their start and end apart: 40, of which 14 were waited for; matrix products, arithmetic and copies ran while one was open for 5% of the time, Pallas kernels for 0%

commit v1 on v0

--- a/solution.py
+++ b/solution.py
@@ -134,7 +134,8 @@
 
     def paired(residual_now, scaled_now, image_now):
         return lax.psum(
-            (jnp.sum(residual_now * scaled_now), jnp.sum(scaled_now * image_now)), ("gx", "gy")
+            lax.psum((jnp.sum(residual_now * scaled_now), jnp.sum(scaled_now * image_now)), "gy"),
+            "gx",
         )
 
     image = apply_stiffness_matrix(scaled, rimmed(scaled))

time: 363 us -> 310 us (0.85)
  blocking collectives: 183 us -> 133 us
  starting transfers between devices: 96.6 us -> 87.9 us
  local copies, waits for them, and re-layouts: 8.88 us -> 13.7 us
    psum x4, blocking collectives: 166 us -> 35.4 us  [paired(): lax.psum((jnp.sum(residual_now * scaled_now), jnp.sum(scaled_now * image_...]
    psum x0 -> x4, blocking collectives: none -> 80 us  [paired(): lax.psum(lax.psum((jnp.sum(residual_now * scaled_now), jnp.sum(scaled_now...]
    ppermute x20, starting transfers between devices: 70.2 us -> 61.6 us  [padded_2(): lax.ppermute(tail, axis, [(i, (i + 1) % count) for i in range(ends)])]
  transfers between devices with their start and end apart: 40 -> 40, of which waited for: 14 -> 14; matrix products, arithmetic and copies ran while one was open for 5% -> 7% of each run, Pallas kernels for 0% -> 0%
where the time goes in v1:
time: 310 us; the launch traced here: 308 us
  blocking collectives  133 us (43%)
  starting transfers between devices  87.9 us (28%)
  waiting for transfers between devices  38.8 us (13%)
  other arithmetic  19.9 us (6%)
  between operations  15.2 us (5%)
  local copies, waits for them, and re-layouts  13.7 us (4%)
    psum x4, blocking collectives, paired(): lax.psum(lax.psum((jnp.sum(residual_now * scaled_now), jnp.sum(scaled_now...  80 us
    ppermute x20, starting transfers between devices, padded_2(): lax.ppermute(tail, axis, [(i, (i + 1) % count) for i in range(ends)])  61.6 us
    ppermute x20, waiting for transfers between devices, padded_2(): lax.ppermute(head, axis, [((i + 1) % count, i) for i in range(ends)])  37.8 us
    psum x4, blocking collectives, paired(): lax.psum((jnp.sum(residual_now * scaled_now), jnp.sum(scaled_now * image_...  35.4 us
    ppermute x20, starting transfers between devices, padded_2(): lax.ppermute(head, axis, [((i + 1) % count, i) for i in range(ends)])  26.3 us
    all_gather x1, blocking collectives, local(): flux_wide = lax.all_gather(flux_mean, 'gy', axis=1, tiled=True)  6.63 us
  transfers between devices with their start and end apart: 40, of which 14 were waited for; matrix products, arithmetic and copies ran while one was open for 7% of the time, Pallas kernels for 0%

profile of v1, /device:TPU:0, one launch (start us, length us, event | category | flops | bytes accessed | tf_op | source)
XLA Modules:
  0.0 308.3 jit_solution(17066482543853057386)
XLA Ops:
  1.6 4.9 %collective-permute-start = (f32[1,16,1024]{2,1,0:T(8,128)S(1)}, f32[1,16,1024]{2,1,0:T(8,128)S(1)}, u32[]{:S(2)}, u32[]{:S(2)}) collective-permute-start(f32[1,16,1024]{2,1,0:T(8,128)S(1)} %get-tuple-element.120), channel_id=1, source_target_pairs={{0,4},{4,8},{8,12},{12,16},{16,20},{20,24},{24,28},{1,5},{5,9},{9,... | collective-permute-start | bytes 196616 | tf_op jit(solution)/shard_map/ppermute | solution.py:19
  6.5 1.4 collective-permute-start.1
  9.9 5.2 %collective-permute-start.17 = (f32[1,16,1024]{2,1,0:T(8,128)S(1)}, f32[1,16,1024]{2,1,0:T(8,128)S(1)}, u32[]{:S(2)}, u32[]{:S(2)}) collective-permute-start(f32[1,16,1024]{2,1,0:T(8,128)S(1)} %get-tuple-element.99), channel_id=1, source_target_pairs={{0,4},{4,8},{8,12},{12,16},{16,20},{20,24},{24,28},{1,5},{5,9},{9,... | collective-permute-start | bytes 196616 | tf_op jit(solution)/shard_map/ppermute | solution.py:19
  15.1 4.8 %collective-permute-start.16 = (f32[1,16,1024]{2,1,0:T(8,128)S(1)}, f32[1,16,1024]{2,1,0:T(8,128)S(1)}, u32[]{:S(2)}, u32[]{:S(2)}) collective-permute-start(f32[1,16,1024]{2,1,0:T(8,128)S(1)} %get-tuple-element.104), channel_id=1, source_target_pairs={{0,4},{4,8},{8,12},{12,16},{16,20},{20,24},{24,28},{1,5},{5,9},{9,... | collective-permute-start | bytes 196616 | tf_op jit(solution)/shard_map/ppermute | solution.py:19
  23.3 5.3 %all-gather.1 = s32[4,16,4]{1,2,0:T(4,128)S(1)} all-gather(s32[1,16,4]{1,2,0:T(4,128)S(1)} %bitcast.80), channel_id=1, replica_groups=mesh['gx'=8,'gy'=4] {'gy'}, dimensions={0}, use_global_device_ids=true | all-gather | bytes 1280 | tf_op jit(solution)/shard_map/all_gather | solution.py:112
  29.3 5.4 %all-gather = f32[4,64,1]{2,1,0:T(8,128)S(1)} all-gather(f32[4,16,1]{2,1,0:T(8,128)S(1)} %slice.433), channel_id=2, replica_groups=mesh['gx'=8,'gy'=4] {'gy'}, dimensions={1}, use_global_device_ids=true | all-gather | bytes 1280 | tf_op jit(solution)/shard_map/all_gather | solution.py:86
  37.7 4.9 %collective-permute-done.18 = f32[1,16,1024]{2,1,0:T(8,128)S(1)} collective-permute-done((f32[1,16,1024]{2,1,0:T(8,128)S(1)}, f32[1,16,1024]{2,1,0:T(8,128)S(1)}, u32[]{:S(2)}, u32[]{:S(2)}) %collective-permute-start.18) | collective-permute-done | bytes 65568 | tf_op jit(solution)/shard_map/ppermute | solution.py:21
  44.6 3.0 collective-permute-start.20
  47.8 3.1 %collective-permute-start.2 = (f32[6,1,1024]{2,1,0:T(1,128)S(1)}, f32[6,1,1024]{2,1,0:T(1,128)S(1)}, u32[]{:S(2)}, u32[]{:S(2)}) collective-permute-start(f32[6,1,1024]{2,1,0:T(1,128)S(1)} %get-tuple-element.78), channel_id=1, source_target_pairs={{0,1},{1,2},{2,3},{4,5},{5,6},{6,7},{8,9},{9,10},{10,11},{12,13},{... | collective-permute-start | bytes 73736 | tf_op jit(solution)/shard_map/ppermute | solution.py:19
  51.0 1.3 collective-permute-start.3
  53.8 3.0 collective-permute-start.21
  57.3 4.3 %collective-permute-start.4 = (f32[1,16,1024]{2,1,0:T(8,128)S(1)}, f32[1,16,1024]{2,1,0:T(8,128)S(1)}, u32[]{:S(2)}, u32[]{:S(2)}) collective-permute-start(f32[1,16,1024]{2,1,0:T(8,128)S(1)} %get-tuple-element.116), channel_id=1, source_target_pairs={{0,4},{4,8},{8,12},{12,16},{16,20},{20,24},{24,28},{1,5},{5,9},{9,... | collective-permute-start | bytes 196616 | tf_op jit(solution)/shard_map/ppermute | solution.py:19
  61.6 1.3 collective-permute-start.5
  63.5 4.5 %collective-permute-done.5 = f32[1,16,1024]{2,1,0:T(8,128)S(1)} collective-permute-done((f32[1,16,1024]{2,1,0:T(8,128)S(1)}, f32[1,16,1024]{2,1,0:T(8,128)S(1)}, u32[]{:S(2)}, u32[]{:S(2)}) %collective-permute-start.5) | collective-permute-done | bytes 65568 | tf_op jit(solution)/shard_map/ppermute | solution.py:21
  68.0 2.2 collective-permute-start.6
  70.2 1.3 collective-permute-start.7
  71.6 2.4 collective-permute-done.7
  74.5 3.4 %collective-permute-start.8 = (f32[1,16,1024]{2,1,0:T(8,128)S(1)}, f32[1,16,1024]{2,1,0:T(8,128)S(1)}, u32[]{:S(2)}, u32[]{:S(2)}) collective-permute-start(f32[1,16,1024]{2,1,0:T(8,128)S(1)} %get-tuple-element.112), channel_id=1, source_target_pairs={{0,4},{4,8},{8,12},{12,16},{16,20},{20,24},{24,28},{1,5},{5,9},{9,... | collective-permute-start | bytes 196616 | tf_op jit(solution)/shard_map/ppermute | solution.py:19
  77.9 1.3 collective-permute-start.9
  79.8 4.3 %collective-permute-done.9 = f32[1,16,1024]{2,1,0:T(8,128)S(1)} collective-permute-done((f32[1,16,1024]{2,1,0:T(8,128)S(1)}, f32[1,16,1024]{2,1,0:T(8,128)S(1)}, u32[]{:S(2)}, u32[]{:S(2)}) %collective-permute-start.9) | collective-permute-done | bytes 65568 | tf_op jit(solution)/shard_map/ppermute | solution.py:21
  84.1 3.0 collective-permute-start.10
  87.1 1.3 collective-permute-start.11
  88.5 1.3 collective-permute-start.23
  89.8 1.3 collective-permute-done.11
  92.2 6.6 %all-gather.2 = f32[4,16,4]{1,2,0:T(4,128)S(1)} all-gather(f32[1,16,4]{1,2,0:T(4,128)S(1)} %multiply_bitcast_fusion), channel_id=1, replica_groups=mesh['gx'=8,'gy'=4] {'gy'}, dimensions={0}, use_global_device_ids=true | all-gather | bytes 1280 | tf_op jit(solution)/shard_map/all_gather | solution.py:113
  101.1 2.8 fusion.162
  103.9 4.3 %collective-permute-start.24 = (f32[1,16,1024]{2,1,0:T(8,128)S(1)}, f32[1,16,1024]{2,1,0:T(8,128)S(1)}, u32[]{:S(2)}, u32[]{:S(2)}) collective-permute-start(f32[1,16,1024]{2,1,0:T(8,128)S(1)} %get-tuple-element.92), channel_id=1, source_target_pairs={{0,4},{4,8},{8,12},{12,16},{16,20},{20,24},{24,28},{1,5},{5,9},{9,... | collective-permute-start | bytes 196616 | tf_op jit(solution)/shard_map/ppermute | solution.py:19
  108.2 1.3 collective-permute-start.25
  110.4 4.0 %collective-permute-done.25 = f32[1,16,1024]{2,1,0:T(8,128)S(1)} collective-permute-done((f32[1,16,1024]{2,1,0:T(8,128)S(1)}, f32[1,16,1024]{2,1,0:T(8,128)S(1)}, u32[]{:S(2)}, u32[]{:S(2)}) %collective-permute-start.25) | collective-permute-done | bytes 65568 | tf_op jit(solution)/shard_map/ppermute | solution.py:21
  114.4 1.3 collective-permute-start.26
  115.7 1.3 collective-permute-start.27
  117.2 3.4 %collective-permute-done.27 = f32[6,1,1024]{2,1,0:T(1,128)S(1)} collective-permute-done((f32[6,1,1024]{2,1,0:T(1,128)S(1)}, f32[6,1,1024]{2,1,0:T(1,128)S(1)}, u32[]{:S(2)}, u32[]{:S(2)}) %collective-permute-start.27) | collective-permute-done | bytes 24608 | tf_op jit(solution)/shard_map/ppermute | solution.py:21
  120.6 1.7 multiply_reduce_fusion.5
  122.3 8.8 %all-reduce.23 = (f32[]{:T(128)}, f32[]{:T(128)}) all-reduce(f32[]{:T(128)} %get-tuple-element.27, f32[]{:T(128)} %get-tuple-element.26), channel_id=1, replica_groups=mesh['gx'=8,'gy'=4] {'gy'}, use_global_device_ids=true, to_apply=%region_3.4 | all-reduce | flops 2 | bytes 16 | tf_op jit(solution)/shard_map/psum | solution.py:137
  131.1 19.3 %all-reduce.19 = (f32[]{:T(128)}, f32[]{:T(128)}) all-reduce(f32[]{:T(128)} %get-tuple-element.42, f32[]{:T(128)} %get-tuple-element.43), channel_id=1, replica_groups=mesh['gx'=8,'gy'=4] {'gx'}, use_global_device_ids=true, to_apply=%region_4.5 | all-reduce | flops 2 | bytes 16 | tf_op jit(solution)/shard_map/psum | solution.py:136
  152.9 2.4 collective-permute-start.28
  155.3 1.3 collective-permute-start.29
  157.3 5.2 %collective-permute-start.12 = (f32[1,16,1024]{2,1,0:T(8,128)}, f32[1,16,1024]{2,1,0:T(8,128)}, u32[]{:S(2)}, u32[]{:S(2)}) collective-permute-start(f32[1,16,1024]{2,1,0:T(8,128)} %get-tuple-element.108), channel_id=1, source_target_pairs={{0,4},{4,8},{8,12},{12,16},{16,20},{20,24},{24,28},{1,5},{5,9},{9,... | collective-permute-start | bytes 196616 | tf_op jit(solution)/shard_map/ppermute | solution.py:19
  163.8 1.3 collective-permute-start.30
  165.1 1.4 collective-permute-start.31
  166.7 3.5 %collective-permute-done.31 = f32[6,1,1024]{2,1,0:T(1,128)S(1)} collective-permute-done((f32[6,1,1024]{2,1,0:T(1,128)S(1)}, f32[6,1,1024]{2,1,0:T(1,128)S(1)}, u32[]{:S(2)}, u32[]{:S(2)}) %collective-permute-start.31) | collective-permute-done | bytes 24608 | tf_op jit(solution)/shard_map/ppermute | solution.py:21
  170.2 1.6 multiply_reduce_fusion.3
  171.9 8.8 %all-reduce.22 = (f32[]{:T(128)}, f32[]{:T(128)}) all-reduce(f32[]{:T(128)} %get-tuple-element.25, f32[]{:T(128)} %get-tuple-element.24), channel_id=1, replica_groups=mesh['gx'=8,'gy'=4] {'gy'}, use_global_device_ids=true, to_apply=%region_9.10 | all-reduce | flops 2 | bytes 16 | tf_op jit(solution)/shard_map/psum | solution.py:137
  180.7 20.4 %all-reduce.18 = (f32[]{:T(128)}, f32[]{:T(128)}) all-reduce(f32[]{:T(128)} %get-tuple-element.40, f32[]{:T(128)} %get-tuple-element.41), channel_id=1, replica_groups=mesh['gx'=8,'gy'=4] {'gx'}, use_global_device_ids=true, to_apply=%region_10.11 | all-reduce | flops 2 | bytes 16 | tf_op jit(solution)/shard_map/psum | solution.py:136
  206.8 1.3 collective-permute-start.32
  208.1 1.3 collective-permute-start.33
  209.5 1.5 pad_maximum_fusion.86
  210.9 1.9 collective-permute-start.14
  214.3 4.1 %collective-permute-start.34 = (f32[6,1,1024]{2,1,0:T(1,128)S(1)}, f32[6,1,1024]{2,1,0:T(1,128)S(1)}, u32[]{:S(2)}, u32[]{:S(2)}) collective-permute-start(f32[6,1,1024]{2,1,0:T(1,128)S(1)} %get-tuple-element.62), channel_id=1, source_target_pairs={{0,1},{1,2},{2,3},{4,5},{5,6},{6,7},{8,9},{9,10},{10,11},{12,13},{... | collective-permute-start | bytes 73736 | tf_op jit(solution)/shard_map/ppermute | solution.py:19
  218.5 1.4 collective-permute-start.35
  220.1 2.9 collective-permute-done.35
  223.0 1.7 multiply_reduce_fusion.1
  224.6 8.9 %all-reduce.21 = (f32[]{:T(128)}, f32[]{:T(128)}) all-reduce(f32[]{:T(128)} %get-tuple-element.23, f32[]{:T(128)} %get-tuple-element.22), channel_id=1, replica_groups=mesh['gx'=8,'gy'=4] {'gy'}, use_global_device_ids=true, to_apply=%region_15.16 | all-reduce | flops 2 | bytes 16 | tf_op jit(solution)/shard_map/psum | solution.py:137
  233.5 20.8 %all-reduce.17 = (f32[]{:T(128)}, f32[]{:T(128)}) all-reduce(f32[]{:T(128)} %get-tuple-element.38, f32[]{:T(128)} %get-tuple-element.39), channel_id=1, replica_groups=mesh['gx'=8,'gy'=4] {'gx'}, use_global_device_ids=true, to_apply=%region_16.17 | all-reduce | flops 2 | bytes 16 | tf_op jit(solution)/shard_map/psum | solution.py:136
  258.1 2.1 multiply_reduce_fusion
  260.2 1.4 collective-permute-start.36
  261.7 1.3 collective-permute-start.37
  263.0 2.0 fusion.91
  265.0 2.8 collective-permute-done.37
  267.9 1.3 collective-permute-start.38
  269.2 1.4 collective-permute-start.39
  270.8 3.5 %collective-permute-done.39 = f32[6,1,1024]{2,1,0:T(1,128)S(1)} collective-permute-done((f32[6,1,1024]{2,1,0:T(1,128)S(1)}, f32[6,1,1024]{2,1,0:T(1,128)S(1)}, u32[]{:S(2)}, u32[]{:S(2)}) %collective-permute-start.39) | collective-permute-done | bytes 24608 | tf_op jit(solution)/shard_map/ppermute | solution.py:21
  275.2 8.9 %all-reduce.20 = (f32[]{:T(128)}, f32[]{:T(128)}) all-reduce(f32[]{:T(128)} %get-tuple-element.44, f32[]{:T(128)} %fusion.6), channel_id=1, replica_groups=mesh['gx'=8,'gy'=4] {'gy'}, use_global_device_ids=true, to_apply=%region_21.22 | all-reduce | flops 2 | bytes 16 | tf_op jit(solution)/shard_map/psum | solution.py:137
  284.1 19.5 %all-reduce.16 = (f32[]{:T(128)}, f32[]{:T(128)}) all-reduce(f32[]{:T(128)} %get-tuple-element.36, f32[]{:T(128)} %get-tuple-element.37), channel_id=1, replica_groups=mesh['gx'=8,'gy'=4] {'gx'}, use_global_device_ids=true, to_apply=%region_22.23 | all-reduce | flops 2 | bytes 16 | tf_op jit(solution)/shard_map/psum | solution.py:136
  (181 shorter events, 28.0 us)
Async XLA Ops:
  0.6 7.3 %copy-start.3 = (f32[4,16,1024]{2,1,0:T(8,128)S(1)}, f32[4,16,1024]{2,1,0:T(8,128)}, u32[]{:S(2)}) copy-start(f32[4,16,1024]{2,1,0:T(8,128)} %param.15) | copy-start | bytes 786436
  0.6 14.4 %copy-start = (f32[4,16,1024]{2,1,0:T(8,128)S(1)}, f32[4,16,1024]{2,1,0:T(8,128)}, u32[]{:S(2)}) copy-start(f32[4,16,1024]{2,1,0:T(8,128)} %param.17) | copy-start | bytes 786436
  1.6 43.0 %collective-permute-start = (f32[1,16,1024]{2,1,0:T(8,128)S(1)}, f32[1,16,1024]{2,1,0:T(8,128)S(1)}, u32[]{:S(2)}, u32[]{:S(2)}) collective-permute-start(f32[1,16,1024]{2,1,0:T(8,128)S(1)} %get-tuple-element.120), channel_id=1, source_target_pairs={{0,4},{4,8},{8,12},{12,16},{16,20},{20,24},{24,28},{1,5},{5,9},{9,... | collective-permute-start | bytes 196616 | tf_op jit(solution)/shard_map/ppermute | solution.py:19
  6.5 13.4 %copy-start.13 = (f32[4,16,1024]{2,1,0:T(8,128)S(1)}, f32[4,16,1024]{2,1,0:T(8,128)}, u32[]{:S(2)}) copy-start(f32[4,16,1024]{2,1,0:T(8,128)} %param.11) | copy-start | bytes 786436
  6.5 41.2 %collective-permute-start.1 = (f32[1,16,1024]{2,1,0:T(8,128)S(1)}, f32[1,16,1024]{2,1,0:T(8,128)S(1)}, u32[]{:S(2)}, u32[]{:S(2)}) collective-permute-start(f32[1,16,1024]{2,1,0:T(8,128)S(1)} %get-tuple-element.121), channel_id=1, source_target_pairs={{4,0},{8,4},{12,8},{16,12},{20,16},{24,20},{28,24},{5,1},{9,5},{13... | collective-permute-start | bytes 196616 | tf_op jit(solution)/shard_map/ppermute | solution.py:21
  8.6 43.8 %collective-permute-start.19 = (f32[1,16,1024]{2,1,0:T(8,128)}, f32[1,16,1024]{2,1,0:T(8,128)S(1)}, u32[]{:S(2)}, u32[]{:S(2)}) collective-permute-start(f32[1,16,1024]{2,1,0:T(8,128)} %get-tuple-element.98), channel_id=1, source_target_pairs={{4,0},{8,4},{12,8},{16,12},{20,16},{24,20},{28,24},{5,1},{9,5},{13... | collective-permute-start | bytes 196616 | tf_op jit(solution)/shard_map/ppermute | solution.py:21
  9.9 41.1 %collective-permute-start.17 = (f32[1,16,1024]{2,1,0:T(8,128)S(1)}, f32[1,16,1024]{2,1,0:T(8,128)S(1)}, u32[]{:S(2)}, u32[]{:S(2)}) collective-permute-start(f32[1,16,1024]{2,1,0:T(8,128)S(1)} %get-tuple-element.99), channel_id=1, source_target_pairs={{0,4},{4,8},{8,12},{12,16},{16,20},{20,24},{24,28},{1,5},{5,9},{9,... | collective-permute-start | bytes 196616 | tf_op jit(solution)/shard_map/ppermute | solution.py:19
  15.1 21.3 %collective-permute-start.16 = (f32[1,16,1024]{2,1,0:T(8,128)S(1)}, f32[1,16,1024]{2,1,0:T(8,128)S(1)}, u32[]{:S(2)}, u32[]{:S(2)}) collective-permute-start(f32[1,16,1024]{2,1,0:T(8,128)S(1)} %get-tuple-element.104), channel_id=1, source_target_pairs={{0,4},{4,8},{8,12},{12,16},{16,20},{20,24},{24,28},{1,5},{5,9},{9,... | collective-permute-start | bytes 196616 | tf_op jit(solution)/shard_map/ppermute | solution.py:19
  23.3 6.0 %copy-start.35 = (s32[4,16,8]{1,2,0:T(8,128)S(1)}, s32[4,16,8]{1,2,0:T(8,128)}, u32[]{:S(2)}) copy-start(s32[4,16,8]{1,2,0:T(8,128)} %param.14) | copy-start | bytes 6148
  35.6 55.6 %copy-start.22 = (f32[4,16,1]{2,1,0:T(8,128)}, f32[4,16,1]{2,1,0:T(8,128)S(1)}, u32[]{:S(2)}) copy-start(f32[4,16,1]{2,1,0:T(8,128)S(1)} %copy.374) | copy-start | bytes 772
  36.4 6.2 %collective-permute-start.18 = (f32[1,16,1024]{2,1,0:T(8,128)S(1)}, f32[1,16,1024]{2,1,0:T(8,128)S(1)}, u32[]{:S(2)}, u32[]{:S(2)}) collective-permute-start(f32[1,16,1024]{2,1,0:T(8,128)S(1)} %get-tuple-element.105), channel_id=1, source_target_pairs={{4,0},{8,4},{12,8},{16,12},{20,16},{24,20},{28,24},{5,1},{9,5},{13... | collective-permute-start | bytes 196616 | tf_op jit(solution)/shard_map/ppermute | solution.py:21
  42.6 5.1 %copy-start.25 = (f32[6,16,1024]{2,1,0:T(8,128)}, f32[6,16,1024]{2,1,0:T(8,128)S(1)}, u32[]{:S(2)}) copy-start(f32[6,16,1024]{2,1,0:T(8,128)S(1)} %constant_dynamic-update-slice_fusion.3) | copy-start | bytes 1179652
  43.3 57.0 %collective-permute-start.22 = (f32[6,1,1024]{2,1,0:T(1,128)}, f32[6,1,1024]{2,1,0:T(1,128)S(1)}, u32[]{:S(2)}, u32[]{:S(2)}) collective-permute-start(f32[6,1,1024]{2,1,0:T(1,128)} %get-tuple-element.68), channel_id=1, source_target_pairs={{1,0},{2,1},{3,2},{5,4},{6,5},{7,6},{9,8},{10,9},{11,10},{13,12},{... | collective-permute-start | bytes 73736 | tf_op jit(solution)/shard_map/ppermute | solution.py:21
  44.6 55.7 %collective-permute-start.20 = (f32[6,1,1024]{2,1,0:T(1,128)}, f32[6,1,1024]{2,1,0:T(1,128)S(1)}, u32[]{:S(2)}, u32[]{:S(2)}) collective-permute-start(f32[6,1,1024]{2,1,0:T(1,128)} %get-tuple-element.69), channel_id=1, source_target_pairs={{0,1},{1,2},{2,3},{4,5},{5,6},{6,7},{8,9},{9,10},{10,11},{12,13},{... | collective-permute-start | bytes 73736 | tf_op jit(solution)/shard_map/ppermute | solution.py:19
  47.7 4.6 %copy-start.28 = (f32[4,16,1024]{2,1,0:T(8,128)S(1)}, f32[4,16,1024]{2,1,0:T(8,128)}, u32[]{:S(2)}) copy-start(f32[4,16,1024]{2,1,0:T(8,128)} %param.18) | copy-start | bytes 786436
  47.7 4.6 %copy-start.2 = (f32[4,16,1024]{2,1,0:T(8,128)S(1)}, f32[4,16,1024]{2,1,0:T(8,128)}, u32[]{:S(2)}) copy-start(f32[4,16,1024]{2,1,0:T(8,128)} %param.16) | copy-start | bytes 786436
  47.8 9.0 %collective-permute-start.2 = (f32[6,1,1024]{2,1,0:T(1,128)S(1)}, f32[6,1,1024]{2,1,0:T(1,128)S(1)}, u32[]{:S(2)}, u32[]{:S(2)}) collective-permute-start(f32[6,1,1024]{2,1,0:T(1,128)S(1)} %get-tuple-element.78), channel_id=1, source_target_pairs={{0,1},{1,2},{2,3},{4,5},{5,6},{6,7},{8,9},{9,10},{10,11},{12,13},{... | collective-permute-start | bytes 73736 | tf_op jit(solution)/shard_map/ppermute | solution.py:19
  51.0 5.8 %collective-permute-start.3 = (f32[6,1,1024]{2,1,0:T(1,128)S(1)}, f32[6,1,1024]{2,1,0:T(1,128)S(1)}, u32[]{:S(2)}, u32[]{:S(2)}) collective-permute-start(f32[6,1,1024]{2,1,0:T(1,128)S(1)} %get-tuple-element.79), channel_id=1, source_target_pairs={{1,0},{2,1},{3,2},{5,4},{6,5},{7,6},{9,8},{10,9},{11,10},{13,12},{... | collective-permute-start | bytes 73736 | tf_op jit(solution)/shard_map/ppermute | solution.py:21
  52.3 4.5 %copy-start.1 = (f32[3,4,16,1024]{3,2,1,0:T(8,128)S(1)}, f32[3,4,16,1024]{3,2,1,0:T(8,128)}, u32[]{:S(2)}) copy-start(f32[3,4,16,1024]{3,2,1,0:T(8,128)} %param.13) | copy-start | bytes 2359300
  52.3 4.5 %copy-start.14 = (f32[4,16,1024]{2,1,0:T(8,128)S(1)}, f32[4,16,1024]{2,1,0:T(8,128)}, u32[]{:S(2)}) copy-start(f32[4,16,1024]{2,1,0:T(8,128)} %param.12) | copy-start | bytes 786436
  53.8 46.6 %collective-permute-start.21 = (f32[6,1,1024]{2,1,0:T(1,128)}, f32[6,1,1024]{2,1,0:T(1,128)S(1)}, u32[]{:S(2)}, u32[]{:S(2)}) collective-permute-start(f32[6,1,1024]{2,1,0:T(1,128)} %get-tuple-element.70), channel_id=1, source_target_pairs={{0,1},{1,2},{2,3},{4,5},{5,6},{6,7},{8,9},{9,10},{10,11},{12,13},{... | collective-permute-start | bytes 73736 | tf_op jit(solution)/shard_map/ppermute | solution.py:19
  57.3 6.2 %collective-permute-start.4 = (f32[1,16,1024]{2,1,0:T(8,128)S(1)}, f32[1,16,1024]{2,1,0:T(8,128)S(1)}, u32[]{:S(2)}, u32[]{:S(2)}) collective-permute-start(f32[1,16,1024]{2,1,0:T(8,128)S(1)} %get-tuple-element.116), channel_id=1, source_target_pairs={{0,4},{4,8},{8,12},{12,16},{16,20},{20,24},{24,28},{1,5},{5,9},{9,... | collective-permute-start | bytes 196616 | tf_op jit(solution)/shard_map/ppermute | solution.py:19
  61.6 6.4 %collective-permute-start.5 = (f32[1,16,1024]{2,1,0:T(8,128)S(1)}, f32[1,16,1024]{2,1,0:T(8,128)S(1)}, u32[]{:S(2)}, u32[]{:S(2)}) collective-permute-start(f32[1,16,1024]{2,1,0:T(8,128)S(1)} %get-tuple-element.117), channel_id=1, source_target_pairs={{4,0},{8,4},{12,8},{16,12},{20,16},{24,20},{28,24},{5,1},{9,5},{13... | collective-permute-start | bytes 196616 | tf_op jit(solution)/shard_map/ppermute | solution.py:21
  68.0 3.6 %collective-permute-start.6 = (f32[6,1,1024]{2,1,0:T(1,128)S(1)}, f32[6,1,1024]{2,1,0:T(1,128)S(1)}, u32[]{:S(2)}, u32[]{:S(2)}) collective-permute-start(f32[6,1,1024]{2,1,0:T(1,128)S(1)} %get-tuple-element.76), channel_id=1, source_target_pairs={{0,1},{1,2},{2,3},{4,5},{5,6},{6,7},{8,9},{9,10},{10,11},{12,13},{... | collective-permute-start | bytes 73736 | tf_op jit(solution)/shard_map/ppermute | solution.py:19
  70.2 3.8 %collective-permute-start.7 = (f32[6,1,1024]{2,1,0:T(1,128)S(1)}, f32[6,1,1024]{2,1,0:T(1,128)S(1)}, u32[]{:S(2)}, u32[]{:S(2)}) collective-permute-start(f32[6,1,1024]{2,1,0:T(1,128)S(1)} %get-tuple-element.77), channel_id=1, source_target_pairs={{1,0},{2,1},{3,2},{5,4},{6,5},{7,6},{9,8},{10,9},{11,10},{13,12},{... | collective-permute-start | bytes 73736 | tf_op jit(solution)/shard_map/ppermute | solution.py:21
  74.5 5.3 %collective-permute-start.8 = (f32[1,16,1024]{2,1,0:T(8,128)S(1)}, f32[1,16,1024]{2,1,0:T(8,128)S(1)}, u32[]{:S(2)}, u32[]{:S(2)}) collective-permute-start(f32[1,16,1024]{2,1,0:T(8,128)S(1)} %get-tuple-element.112), channel_id=1, source_target_pairs={{0,4},{4,8},{8,12},{12,16},{16,20},{20,24},{24,28},{1,5},{5,9},{9,... | collective-permute-start | bytes 196616 | tf_op jit(solution)/shard_map/ppermute | solution.py:19
  77.9 6.2 %collective-permute-start.9 = (f32[1,16,1024]{2,1,0:T(8,128)S(1)}, f32[1,16,1024]{2,1,0:T(8,128)S(1)}, u32[]{:S(2)}, u32[]{:S(2)}) collective-permute-start(f32[1,16,1024]{2,1,0:T(8,128)S(1)} %get-tuple-element.113), channel_id=1, source_target_pairs={{4,0},{8,4},{12,8},{16,12},{20,16},{24,20},{28,24},{5,1},{9,5},{13... | collective-permute-start | bytes 196616 | tf_op jit(solution)/shard_map/ppermute | solution.py:21
  84.1 4.4 %collective-permute-start.10 = (f32[6,1,1024]{2,1,0:T(1,128)S(1)}, f32[6,1,1024]{2,1,0:T(1,128)S(1)}, u32[]{:S(2)}, u32[]{:S(2)}) collective-permute-start(f32[6,1,1024]{2,1,0:T(1,128)S(1)} %get-tuple-element.74), channel_id=1, source_target_pairs={{0,1},{1,2},{2,3},{4,5},{5,6},{6,7},{8,9},{9,10},{10,11},{12,13},{... | collective-permute-start | bytes 73736 | tf_op jit(solution)/shard_map/ppermute | solution.py:19
  87.1 4.0 %collective-permute-start.11 = (f32[6,1,1024]{2,1,0:T(1,128)S(1)}, f32[6,1,1024]{2,1,0:T(1,128)S(1)}, u32[]{:S(2)}, u32[]{:S(2)}) collective-permute-start(f32[6,1,1024]{2,1,0:T(1,128)S(1)} %get-tuple-element.75), channel_id=1, source_target_pairs={{1,0},{2,1},{3,2},{5,4},{6,5},{7,6},{9,8},{10,9},{11,10},{13,12},{... | collective-permute-start | bytes 73736 | tf_op jit(solution)/shard_map/ppermute | solution.py:21
  88.5 11.9 %collective-permute-start.23 = (f32[6,1,1024]{2,1,0:T(1,128)}, f32[6,1,1024]{2,1,0:T(1,128)S(1)}, u32[]{:S(2)}, u32[]{:S(2)}) collective-permute-start(f32[6,1,1024]{2,1,0:T(1,128)} %get-tuple-element.71), channel_id=1, source_target_pairs={{1,0},{2,1},{3,2},{5,4},{6,5},{7,6},{9,8},{10,9},{11,10},{13,12},{... | collective-permute-start | bytes 73736 | tf_op jit(solution)/shard_map/ppermute | solution.py:21
  103.8 16.8 %copy-start.9 = (f32[4,16,1024]{2,1,0:T(8,128)}, f32[4,16,1024]{2,1,0:T(8,128)S(1)}, u32[]{:S(2)}) copy-start(f32[4,16,1024]{2,1,0:T(8,128)S(1)} %get-tuple-element.59) | copy-start | bytes 786436
  103.8 16.8 %copy-start.16 = (f32[4,16,1024]{2,1,0:T(8,128)}, f32[4,16,1024]{2,1,0:T(8,128)S(1)}, u32[]{:S(2)}) copy-start(f32[4,16,1024]{2,1,0:T(8,128)S(1)} %get-tuple-element.55) | copy-start | bytes 786436
  103.9 66.4 %copy-start.6 = (f32[4,16,1024]{2,1,0:T(8,128)}, f32[4,16,1024]{2,1,0:T(8,128)S(1)}, u32[]{:S(2)}) copy-start(f32[4,16,1024]{2,1,0:T(8,128)S(1)} %get-tuple-element.58) | copy-start | bytes 786436
  103.9 119.1 %copy-start.4 = (f32[4,16,1024]{2,1,0:T(8,128)}, f32[4,16,1024]{2,1,0:T(8,128)S(1)}, u32[]{:S(2)}) copy-start(f32[4,16,1024]{2,1,0:T(8,128)S(1)} %get-tuple-element.57) | copy-start | bytes 786436
  103.9 6.5 %collective-permute-start.24 = (f32[1,16,1024]{2,1,0:T(8,128)S(1)}, f32[1,16,1024]{2,1,0:T(8,128)S(1)}, u32[]{:S(2)}, u32[]{:S(2)}) collective-permute-start(f32[1,16,1024]{2,1,0:T(8,128)S(1)} %get-tuple-element.92), channel_id=1, source_target_pairs={{0,4},{4,8},{8,12},{12,16},{16,20},{20,24},{24,28},{1,5},{5,9},{9,... | collective-permute-start | bytes 196616 | tf_op jit(solution)/shard_map/ppermute | solution.py:19
  108.2 6.2 %collective-permute-start.25 = (f32[1,16,1024]{2,1,0:T(8,128)S(1)}, f32[1,16,1024]{2,1,0:T(8,128)S(1)}, u32[]{:S(2)}, u32[]{:S(2)}) collective-permute-start(f32[1,16,1024]{2,1,0:T(8,128)S(1)} %get-tuple-element.93), channel_id=1, source_target_pairs={{4,0},{8,4},{12,8},{16,12},{20,16},{24,20},{28,24},{5,1},{9,5},{13... | collective-permute-start | bytes 196616 | tf_op jit(solution)/shard_map/ppermute | solution.py:21
  114.4 2.7 collective-permute-start.26
  115.7 4.9 %collective-permute-start.27 = (f32[6,1,1024]{2,1,0:T(1,128)S(1)}, f32[6,1,1024]{2,1,0:T(1,128)S(1)}, u32[]{:S(2)}, u32[]{:S(2)}) collective-permute-start(f32[6,1,1024]{2,1,0:T(1,128)S(1)} %get-tuple-element.67), channel_id=1, source_target_pairs={{1,0},{2,1},{3,2},{5,4},{6,5},{7,6},{9,8},{10,9},{11,10},{13,12},{... | collective-permute-start | bytes 73736 | tf_op jit(solution)/shard_map/ppermute | solution.py:21
  152.9 17.3 %copy-start.17 = (f32[4,16,1024]{2,1,0:T(8,128)}, f32[4,16,1024]{2,1,0:T(8,128)S(1)}, u32[]{:S(2)}) copy-start(f32[4,16,1024]{2,1,0:T(8,128)S(1)} %get-tuple-element.51) | copy-start | bytes 786436
  152.9 10.8 %collective-permute-start.28 = (f32[1,16,1024]{2,1,0:T(8,128)S(1)}, f32[1,16,1024]{2,1,0:T(8,128)S(1)}, u32[]{:S(2)}, u32[]{:S(2)}) collective-permute-start(f32[1,16,1024]{2,1,0:T(8,128)S(1)} %get-tuple-element.88), channel_id=1, source_target_pairs={{0,4},{4,8},{8,12},{12,16},{16,20},{20,24},{24,28},{1,5},{5,9},{9,... | collective-permute-start | bytes 196616 | tf_op jit(solution)/shard_map/ppermute | solution.py:19
  155.3 8.4 %collective-permute-start.29 = (f32[1,16,1024]{2,1,0:T(8,128)S(1)}, f32[1,16,1024]{2,1,0:T(8,128)S(1)}, u32[]{:S(2)}, u32[]{:S(2)}) collective-permute-start(f32[1,16,1024]{2,1,0:T(8,128)S(1)} %get-tuple-element.89), channel_id=1, source_target_pairs={{4,0},{8,4},{12,8},{16,12},{20,16},{24,20},{28,24},{5,1},{9,5},{13... | collective-permute-start | bytes 196616 | tf_op jit(solution)/shard_map/ppermute | solution.py:21
  157.3 52.1 %collective-permute-start.12 = (f32[1,16,1024]{2,1,0:T(8,128)}, f32[1,16,1024]{2,1,0:T(8,128)}, u32[]{:S(2)}, u32[]{:S(2)}) collective-permute-start(f32[1,16,1024]{2,1,0:T(8,128)} %get-tuple-element.108), channel_id=1, source_target_pairs={{0,4},{4,8},{8,12},{12,16},{16,20},{20,24},{24,28},{1,5},{5,9},{9,... | collective-permute-start | bytes 196616 | tf_op jit(solution)/shard_map/ppermute | solution.py:19
  162.5 47.0 %collective-permute-start.13 = (f32[1,16,1024]{2,1,0:T(8,128)}, f32[1,16,1024]{2,1,0:T(8,128)}, u32[]{:S(2)}, u32[]{:S(2)}) collective-permute-start(f32[1,16,1024]{2,1,0:T(8,128)} %get-tuple-element.109), channel_id=1, source_target_pairs={{4,0},{8,4},{12,8},{16,12},{20,16},{24,20},{28,24},{5,1},{9,5},{13... | collective-permute-start | bytes 196616 | tf_op jit(solution)/shard_map/ppermute | solution.py:21
  163.8 2.9 collective-permute-start.30
  165.1 5.1 %copy-start.10 = (f32[4,16,1024]{2,1,0:T(8,128)S(1)}, f32[4,16,1024]{2,1,0:T(8,128)}, u32[]{:S(2)}) copy-start(f32[4,16,1024]{2,1,0:T(8,128)} %copy-done.9) | copy-start | bytes 786436
  165.1 5.1 %collective-permute-start.31 = (f32[6,1,1024]{2,1,0:T(1,128)S(1)}, f32[6,1,1024]{2,1,0:T(1,128)S(1)}, u32[]{:S(2)}, u32[]{:S(2)}) collective-permute-start(f32[6,1,1024]{2,1,0:T(1,128)S(1)} %get-tuple-element.65), channel_id=1, source_target_pairs={{1,0},{2,1},{3,2},{5,4},{6,5},{7,6},{9,8},{10,9},{11,10},{13,12},{... | collective-permute-start | bytes 73736 | tf_op jit(solution)/shard_map/ppermute | solution.py:21
  206.8 16.2 %copy-start.18 = (f32[4,16,1024]{2,1,0:T(8,128)}, f32[4,16,1024]{2,1,0:T(8,128)S(1)}, u32[]{:S(2)}) copy-start(f32[4,16,1024]{2,1,0:T(8,128)S(1)} %get-tuple-element.48) | copy-start | bytes 786436
  206.8 7.2 %collective-permute-start.32 = (f32[1,16,1024]{2,1,0:T(8,128)S(1)}, f32[1,16,1024]{2,1,0:T(8,128)S(1)}, u32[]{:S(2)}, u32[]{:S(2)}) collective-permute-start(f32[1,16,1024]{2,1,0:T(8,128)S(1)} %get-tuple-element.84), channel_id=1, source_target_pairs={{0,4},{4,8},{8,12},{12,16},{16,20},{20,24},{24,28},{1,5},{5,9},{9,... | collective-permute-start | bytes 196616 | tf_op jit(solution)/shard_map/ppermute | solution.py:19
  208.1 6.2 %collective-permute-start.33 = (f32[1,16,1024]{2,1,0:T(8,128)S(1)}, f32[1,16,1024]{2,1,0:T(8,128)S(1)}, u32[]{:S(2)}, u32[]{:S(2)}) collective-permute-start(f32[1,16,1024]{2,1,0:T(8,128)S(1)} %get-tuple-element.85), channel_id=1, source_target_pairs={{4,0},{8,4},{12,8},{16,12},{20,16},{24,20},{28,24},{5,1},{9,5},{13... | collective-permute-start | bytes 196616 | tf_op jit(solution)/shard_map/ppermute | solution.py:21
  210.9 52.0 %collective-permute-start.14 = (f32[6,1,1024]{2,1,0:T(1,128)}, f32[6,1,1024]{2,1,0:T(1,128)}, u32[]{:S(2)}, u32[]{:S(2)}) collective-permute-start(f32[6,1,1024]{2,1,0:T(1,128)} %get-tuple-element.72), channel_id=1, source_target_pairs={{0,1},{1,2},{2,3},{4,5},{5,6},{6,7},{8,9},{9,10},{10,11},{12,13},{... | collective-permute-start | bytes 73736 | tf_op jit(solution)/shard_map/ppermute | solution.py:19
  212.8 50.2 %collective-permute-start.15 = (f32[6,1,1024]{2,1,0:T(1,128)}, f32[6,1,1024]{2,1,0:T(1,128)}, u32[]{:S(2)}, u32[]{:S(2)}) collective-permute-start(f32[6,1,1024]{2,1,0:T(1,128)} %get-tuple-element.73), channel_id=1, source_target_pairs={{1,0},{2,1},{3,2},{5,4},{6,5},{7,6},{9,8},{10,9},{11,10},{13,12},{... | collective-permute-start | bytes 73736 | tf_op jit(solution)/shard_map/ppermute | solution.py:21
  214.3 5.7 %collective-permute-start.34 = (f32[6,1,1024]{2,1,0:T(1,128)S(1)}, f32[6,1,1024]{2,1,0:T(1,128)S(1)}, u32[]{:S(2)}, u32[]{:S(2)}) collective-permute-start(f32[6,1,1024]{2,1,0:T(1,128)S(1)} %get-tuple-element.62), channel_id=1, source_target_pairs={{0,1},{1,2},{2,3},{4,5},{5,6},{6,7},{8,9},{9,10},{10,11},{12,13},{... | collective-permute-start | bytes 73736 | tf_op jit(solution)/shard_map/ppermute | solution.py:19
  218.5 4.5 %copy-start.7 = (f32[4,16,1024]{2,1,0:T(8,128)S(1)}, f32[4,16,1024]{2,1,0:T(8,128)}, u32[]{:S(2)}) copy-start(f32[4,16,1024]{2,1,0:T(8,128)} %copy-done.6) | copy-start | bytes 786436
  218.5 4.5 %collective-permute-start.35 = (f32[6,1,1024]{2,1,0:T(1,128)S(1)}, f32[6,1,1024]{2,1,0:T(1,128)S(1)}, u32[]{:S(2)}, u32[]{:S(2)}) collective-permute-start(f32[6,1,1024]{2,1,0:T(1,128)S(1)} %get-tuple-element.63), channel_id=1, source_target_pairs={{1,0},{2,1},{3,2},{5,4},{6,5},{7,6},{9,8},{10,9},{11,10},{13,12},{... | collective-permute-start | bytes 73736 | tf_op jit(solution)/shard_map/ppermute | solution.py:21
  258.1 4.9 %copy-start.20 = (f32[4,16,1023]{2,1,0:T(8,128)S(1)}, f32[4,16,1023]{2,1,0:T(8,128)}, u32[]{:S(2)}) copy-start(f32[4,16,1023]{2,1,0:T(8,128)} %get-tuple-element.106) | copy-start | bytes 785668
  258.1 4.9 %copy-start.21 = (f32[4,16,1023]{2,1,0:T(8,128)S(1)}, f32[4,16,1023]{2,1,0:T(8,128)}, u32[]{:S(2)}) copy-start(f32[4,16,1023]{2,1,0:T(8,128)} %get-tuple-element.107) | copy-start | bytes 785668
  258.1 4.9 %copy-start.23 = (f32[4,16,1]{2,1,0:T(8,128)S(1)}, f32[4,16,1]{2,1,0:T(8,128)}, u32[]{:S(2)}) copy-start(f32[4,16,1]{2,1,0:T(8,128)} %copy-done.22) | copy-start | bytes 772
  260.2 4.8 %collective-permute-start.36 = (f32[1,16,1024]{2,1,0:T(8,128)S(1)}, f32[1,16,1024]{2,1,0:T(8,128)S(1)}, u32[]{:S(2)}, u32[]{:S(2)}) collective-permute-start(f32[1,16,1024]{2,1,0:T(8,128)S(1)} %get-tuple-element.82), channel_id=1, source_target_pairs={{0,4},{4,8},{8,12},{12,16},{16,20},{20,24},{24,28},{1,5},{5,9},{9,... | collective-permute-start | bytes 196616 | tf_op jit(solution)/shard_map/ppermute | solution.py:19
  261.7 6.2 %collective-permute-start.37 = (f32[1,16,1024]{2,1,0:T(8,128)S(1)}, f32[1,16,1024]{2,1,0:T(8,128)S(1)}, u32[]{:S(2)}, u32[]{:S(2)}) collective-permute-start(f32[1,16,1024]{2,1,0:T(8,128)S(1)} %get-tuple-element.83), channel_id=1, source_target_pairs={{4,0},{8,4},{12,8},{16,12},{20,16},{24,20},{28,24},{5,1},{9,5},{13... | collective-permute-start | bytes 196616 | tf_op jit(solution)/shard_map/ppermute | solution.py:21
  267.9 2.9 collective-permute-start.38
  269.2 5.1 %copy-start.5 = (f32[4,16,1024]{2,1,0:T(8,128)S(1)}, f32[4,16,1024]{2,1,0:T(8,128)}, u32[]{:S(2)}) copy-start(f32[4,16,1024]{2,1,0:T(8,128)} %copy-done.4) | copy-start | bytes 786436
  269.2 5.1 %copy-start.8 = (f32[4,16,1024]{2,1,0:T(8,128)S(1)}, f32[4,16,1024]{2,1,0:T(8,128)}, u32[]{:S(2)}) copy-start(f32[4,16,1024]{2,1,0:T(8,128)} %copy-done.6) | copy-start | bytes 786436
  269.2 5.1 %copy-start.12 = (f32[4,16,1024]{2,1,0:T(8,128)S(1)}, f32[4,16,1024]{2,1,0:T(8,128)}, u32[]{:S(2)}) copy-start(f32[4,16,1024]{2,1,0:T(8,128)} %copy-done.9) | copy-start | bytes 786436
  269.2 5.1 %collective-permute-start.39 = (f32[6,1,1024]{2,1,0:T(1,128)S(1)}, f32[6,1,1024]{2,1,0:T(1,128)S(1)}, u32[]{:S(2)}, u32[]{:S(2)}) collective-permute-start(f32[6,1,1024]{2,1,0:T(1,128)S(1)} %get-tuple-element.61), channel_id=1, source_target_pairs={{1,0},{2,1},{3,2},{5,4},{6,5},{7,6},{9,8},{10,9},{11,10},{13,12},{... | collective-permute-start | bytes 73736 | tf_op jit(solution)/shard_map/ppermute | solution.py:21
  (16 other events, 20.3 us)
